TPU v7x, 16 devices: a whole 2x2x2 slice. The times are simulated.
16 devices in a mesh: tp: 2 (over z), side: 2 (over y), rep: 4 (over x, core).
Axes of the slice: x: 2, y: 2, z: 2, core: 2. Of those that a mesh axis runs over, the one named last changes fastest.
Arguments:
- w_up: float32 [2, 6, 896, 4864], P('side', None, ('rep', 'tp'))
- w_down: float32 [2, 6, 4864, 896], P('side', None, None, ('rep', 'tp'))
- g_up: float32 [2, 6, 896, 4864], P('side', None, ('rep', 'tp'))
- g_down: float32 [2, 6, 4864, 896], P('side', None, None, ('rep', 'tp'))
- learn_rate: float32 [2], P('side')
- prompts: bfloat16 [2, 4, 8192, 896], P('side', 'rep')
Outputs:
- output 1: float32 [2, 6, 896, 4864], P('side', None, ('rep', 'tp'))
- output 2: float32 [2, 6, 4864, 896], P('side', None, None, ('rep', 'tp'))
- output 3: bfloat16 [2, 4, 8192, 896], P('side', 'rep')
All inputs are finite; a program needn't handle non-finite values.
Results may differ from a plain program's by a relative error of at most 0.0155867.
Values are sent between devices in bfloat16 or wider.
A program may use at most 1 GiB of HBM per device.

v0:
```python
import jax
import jax.numpy as jnp
from jax import lax
from jax.sharding import PartitionSpec as P


def solution(mesh):
    up_spec = P("side", None, ("rep", "tp"), None)
    down_spec = P("side", None, None, ("rep", "tp"))
    tok_spec = P("side", "rep", None, None)

    def device_step(w_up, w_down, g_up, g_down, learn_rate, prompts):
        is_trainer = lax.axis_index("side") == 0
        rate = learn_rate[0]
        new_up = jnp.where(is_trainer, w_up - rate * g_up, 0.0)
        new_down = jnp.where(is_trainer, w_down - rate * g_down, 0.0)
        recv_up = lax.ppermute(new_up[0].astype(jnp.bfloat16), "side", perm=[(0, 1)])
        recv_down = lax.ppermute(new_down[0].astype(jnp.bfloat16), "side", perm=[(0, 1)])
        band_up = lax.all_to_all(recv_up, "tp", 2, 1, tiled=True)
        band_down = lax.all_to_all(recv_down, "tp", 1, 2, tiled=True)
        full_up = lax.all_gather(band_up, "rep", axis=1, tiled=True)
        full_down = lax.all_gather(band_down, "rep", axis=2, tiled=True)
        hidden = prompts[0, 0]
        for layer in range(full_up.shape[0]):
            pre_act = jnp.dot(hidden, full_up[layer], preferred_element_type=jnp.float32)
            act_up = jax.nn.gelu(pre_act, approximate=True).astype(jnp.bfloat16)
            part_sum = jnp.dot(act_up, full_down[layer], preferred_element_type=jnp.float32)
            part_sum = lax.psum(part_sum, "tp")
            hidden = (hidden.astype(jnp.float32) + part_sum).astype(jnp.bfloat16)
        gen_out = jnp.where(is_trainer, jnp.zeros_like(hidden), hidden)
        return new_up, new_down, gen_out[None, None]

    return jax.shard_map(
        device_step,
        mesh=mesh,
        in_specs=(up_spec, down_spec, up_spec, down_spec, P("side"), tok_spec),
        out_specs=(up_spec, down_spec, tok_spec),
        check_vma=False,
    )
```

profile of v0, /device:TPU:0, one launch (start us, length us, event | category | flops | bytes accessed | tf_op | source)
XLA Modules:
  0.0 5419.4 jit_solution(7625061739362220254)
XLA Ops:
  7.2 0.0 all-gather.3.cloned.1.call-start
  7.9 14.4 convert_bitcast_fusion.1
  22.3 7.9 collective-permute-start
  30.2 137.3 %collective-permute-done = bf16[6,112,4864]{2,1,0:T(8,128)(2,1)} collective-permute-done((bf16[6,112,4864]{2,1,0:T(8,128)(2,1)S(1)}, bf16[6,112,4864]{2,1,0:T(8,128)(2,1)}, u32[]{:S(2)}, u32[]{:S(2)}) %collective-permute-start) | collective-permute-done | bytes 6537248 | tf_op jit(solution)/shard_map/ppermute | solution.py:17
  167.5 13.1 copy.121
  180.5 120.7 %all_to_all.36 = bf16[6,112,4864]{1,0,2:T(8,128)(2,1)} all-to-all(bf16[6,112,4864]{1,0,2:T(8,128)(2,1)} %copy.121), channel_id=1, replica_groups=mesh['tp'=2,'side'=2,'rep'=4] {'tp'}, dimensions={2} | all-to-all | bytes 13074432 | tf_op jit(solution)/shard_map/all_to_all | solution.py:19
  301.2 16.6 copy.157
  317.8 6.3 copy.123
  324.1 0.0 all-gather.3.cloned.1.call-update
  324.1 0.0 all-gather.5.cloned.1.call-start
  324.2 14.4 convert_bitcast_fusion
  338.6 7.2 collective-permute-start.1
  345.8 135.8 %collective-permute-done.1 = bf16[6,4864,112]{1,2,0:T(8,128)(2,1)} collective-permute-done((bf16[6,4864,112]{1,2,0:T(8,128)(2,1)S(1)}, bf16[6,4864,112]{1,2,0:T(8,128)(2,1)}, u32[]{:S(2)}, u32[]{:S(2)}) %collective-permute-start.1) | collective-permute-done | bytes 6537248 | tf_op jit(solution)/shard_map/ppermute | solution.py:18
  481.6 13.1 copy.124
  494.7 119.2 %all_to_all.37 = bf16[6,4864,112]{2,0,1:T(8,128)(2,1)} all-to-all(bf16[6,4864,112]{2,0,1:T(8,128)(2,1)} %copy.124), channel_id=1, replica_groups=mesh['tp'=2,'side'=2,'rep'=4] {'tp'}, dimensions={1} | all-to-all | bytes 13074432 | tf_op jit(solution)/shard_map/all_to_all | solution.py:20
  613.9 16.6 copy.158
  630.5 6.3 copy.126
  636.7 0.0 all-gather.5.cloned.1.call-update
  636.7 0.4 all-reduce.7.cloned.1.call-start
  637.2 0.0 all-gather.3.cloned.1.call-done
  637.2 59.8 %fusion.7.clone.5 = bf16[8192,2432]{0,1:T(8,128)(2,1)} fusion(bf16[1,1,8192,896]{3,2,1,0:T(8,128)(2,1)} %param.11, bf16[6,896,2432]{2,1,0:T(8,128)(2,1)} %all-gather.3.cloned.1.call-done), kind=kOutput, calls=%fused_computation.13.clone.clone.clone.2 | convolution fusion | flops 35881222144 | bytes 58884096 | tf_op jit(solution)/shard_map/dot_general | solution.py:25
  697.0 99.0 %all-gather.5.cloned.1.call-done = bf16[6,2432,896]{1,2,0:T(8,128)(2,1)} async-done(((bf16[6,2432,224]{1,2,0:T(8,128)(2,1)}), bf16[6,2432,896]{1,2,0:T(8,128)(2,1)}) %all-gather.5.cloned.1.call-update) | async-done | bytes 26148880 | tf_op jit(solution)/shard_map/all_gather | solution.py:22
  796.0 61.5 %fusion.52 = f32[8192,896]{1,0:T(8,128)} fusion(bf16[6,2432,896]{1,2,0:T(8,128)(2,1)} %all-gather.5.cloned.1.call-done, bf16[8192,2432]{0,1:T(8,128)(2,1)} %fusion.7.clone.5), kind=kOutput, calls=%fused_computation.63 | convolution fusion | flops 35701915648 | bytes 73564160 | tf_op jit(solution)/shard_map/dot_general | solution.py:27
  857.5 0.0 all-reduce.7.cloned.1.call-update
  857.6 0.0 all-reduce.9.cloned.1.call-start
  857.6 643.9 %all-reduce.7.cloned.1.call-done = f32[8192,896]{1,0:T(8,128)} async-done(((f32[8192,896]{1,0:T(8,128)}), f32[8192,896]{1,0:T(8,128)}) %all-reduce.7.cloned.1.call-update) | async-done | bytes 29360144 | tf_op jit(solution)/shard_map/psum | solution.py:28
  1501.5 71.3 %fusion.15.clone.5 = bf16[8192,2432]{0,1:T(8,128)(2,1)} fusion(bf16[6,896,2432]{2,1,0:T(8,128)(2,1)} %all-gather.3.cloned.1.call-done, f32[8192,896]{1,0:T(8,128)} %all-reduce.7.cloned.1.call-done, bf16[1,1,8192,896]{3,2,1,0:T(8,128)(2,1)} %param.11), kind=kOutput, calls=%fused_computation.21.clone.clone.clone.2 | convolution fusion | flops 35903242240 | bytes 88244224 | tf_op jit(solution)/shard_map/dot_general | solution.py:25
  1572.7 50.7 fusion.58
  1623.5 0.0 all-reduce.9.cloned.1.call-update
  1623.5 0.0 all-reduce.11.cloned.1.call-start
  1623.5 643.8 %all-reduce.9.cloned.1.call-done = f32[8192,896]{1,0:T(8,128)} async-done(((f32[8192,896]{1,0:T(8,128)}), f32[8192,896]{1,0:T(8,128)}) %all-reduce.9.cloned.1.call-update) | async-done | bytes 29360144 | tf_op jit(solution)/shard_map/psum | solution.py:28
  2267.4 28.8 add_convert_fusion.4
  2296.2 69.1 %fusion.23.clone.5 = bf16[8192,2432]{0,1:T(8,128)(2,1)} fusion(bf16[8192,896]{1,0:T(8,128)(2,1)} %add_convert_fusion.4, bf16[6,896,2432]{2,1,0:T(8,128)(2,1)} %all-gather.3.cloned.1.call-done), kind=kOutput, calls=%fused_computation.29.clone.clone.clone.2 | convolution fusion | flops 35881222144 | bytes 58884096 | tf_op jit(solution)/shard_map/dot_general | solution.py:25
  2365.3 50.3 fusion.57
  2415.6 0.0 all-reduce.11.cloned.1.call-update
  2415.6 0.0 all-reduce.13.cloned.1.call-start
  2415.7 643.8 %all-reduce.11.cloned.1.call-done = f32[8192,896]{1,0:T(8,128)} async-done(((f32[8192,896]{1,0:T(8,128)}), f32[8192,896]{1,0:T(8,128)}) %all-reduce.11.cloned.1.call-update) | async-done | bytes 29360144 | tf_op jit(solution)/shard_map/psum | solution.py:28
  3059.5 71.4 %fusion.31.clone.5 = bf16[8192,2432]{0,1:T(8,128)(2,1)} fusion(bf16[6,896,2432]{2,1,0:T(8,128)(2,1)} %all-gather.3.cloned.1.call-done, f32[8192,896]{1,0:T(8,128)} %all-reduce.11.cloned.1.call-done, bf16[8192,896]{1,0:T(8,128)(2,1)} %add_convert_fusion.4), kind=kOutput, calls=%fused_computation.37.clone.clone.clone.2 | convolution fusion | flops 35903242240 | bytes 88244224 | tf_op jit(solution)/shard_map/dot_general | solution.py:25
  3130.9 50.7 fusion.56
  3181.6 0.0 all-reduce.13.cloned.1.call-update
  3181.6 0.0 all-reduce.15.cloned.1.call-start
  3181.7 643.8 %all-reduce.13.cloned.1.call-done = f32[8192,896]{1,0:T(8,128)} async-done(((f32[8192,896]{1,0:T(8,128)}), f32[8192,896]{1,0:T(8,128)}) %all-reduce.13.cloned.1.call-update) | async-done | bytes 29360144 | tf_op jit(solution)/shard_map/psum | solution.py:28
  3825.5 28.8 add_convert_fusion.2
  3854.3 69.1 %fusion.39.clone.5 = bf16[8192,2432]{0,1:T(8,128)(2,1)} fusion(bf16[8192,896]{1,0:T(8,128)(2,1)} %add_convert_fusion.2, bf16[6,896,2432]{2,1,0:T(8,128)(2,1)} %all-gather.3.cloned.1.call-done), kind=kOutput, calls=%fused_computation.45.clone.clone.clone.2 | convolution fusion | flops 35881222144 | bytes 58884096 | tf_op jit(solution)/shard_map/dot_general | solution.py:25
  3923.4 50.3 fusion.55
  3973.7 0.0 all-reduce.15.cloned.1.call-update
  3973.8 0.0 all-reduce.17.cloned.1.call-start
  3973.8 643.8 %all-reduce.15.cloned.1.call-done = f32[8192,896]{1,0:T(8,128)} async-done(((f32[8192,896]{1,0:T(8,128)}), f32[8192,896]{1,0:T(8,128)}) %all-reduce.15.cloned.1.call-update) | async-done | bytes 29360144 | tf_op jit(solution)/shard_map/psum | solution.py:28
  4617.6 71.3 %fusion.47.clone.5 = bf16[8192,2432]{0,1:T(8,128)(2,1)} fusion(bf16[6,896,2432]{2,1,0:T(8,128)(2,1)} %all-gather.3.cloned.1.call-done, f32[8192,896]{1,0:T(8,128)} %all-reduce.15.cloned.1.call-done, bf16[8192,896]{1,0:T(8,128)(2,1)} %add_convert_fusion.2), kind=kOutput, calls=%fused_computation.53.clone.clone.clone.2 | convolution fusion | flops 35903242240 | bytes 88244224 | tf_op jit(solution)/shard_map/dot_general | solution.py:25
  4688.9 50.5 fusion.54
  4739.4 0.0 all-reduce.17.cloned.1.call-update
  4739.5 643.9 %all-reduce.17.cloned.1.call-done = f32[8192,896]{1,0:T(8,128)} async-done(((f32[8192,896]{1,0:T(8,128)}), f32[8192,896]{1,0:T(8,128)}) %all-reduce.17.cloned.1.call-update) | async-done | bytes 29360144 | tf_op jit(solution)/shard_map/psum | solution.py:28
  5383.3 28.9 fusion.49
Async XLA Ops:
  7.2 630.0 %all-gather.3.cloned.1.call-start = ((), (), s32[]{:S(2)}) async-start(), calls=%async_computation.2 | async-start | bytes 32686080 | tf_op jit(solution)/shard_map/all_gather | solution.py:21
  22.3 145.2 %collective-permute-start = (bf16[6,112,4864]{2,1,0:T(8,128)(2,1)S(1)}, bf16[6,112,4864]{2,1,0:T(8,128)(2,1)}, u32[]{:S(2)}, u32[]{:S(2)}) collective-permute-start(bf16[6,112,4864]{2,1,0:T(8,128)(2,1)S(1)} %get-tuple-element.6), channel_id=1, source_target_pairs={{0,4},{1,5},{2,6},{3,7},{8,12},{9,13},{10,14},{11,15}} | collective-permute-start | bytes 19611656 | tf_op jit(solution)/shard_map/ppermute | solution.py:17
  324.1 471.9 %all-gather.5.cloned.1.call-start = ((), (), s32[]{:S(2)}) async-start(), calls=%async_computation.3 | async-start | bytes 32686080 | tf_op jit(solution)/shard_map/all_gather | solution.py:22
  338.6 143.0 %collective-permute-start.1 = (bf16[6,4864,112]{1,2,0:T(8,128)(2,1)S(1)}, bf16[6,4864,112]{1,2,0:T(8,128)(2,1)}, u32[]{:S(2)}, u32[]{:S(2)}) collective-permute-start(bf16[6,4864,112]{1,2,0:T(8,128)(2,1)S(1)} %get-tuple-element.8), channel_id=1, source_target_pairs={{0,4},{1,5},{2,6},{3,7},{8,12},{9,13},{10,14},{11,15}} | collective-permute-start | bytes 19611656 | tf_op jit(solution)/shard_map/ppermute | solution.py:18
  636.7 864.7 %all-reduce.7.cloned.1.call-start = ((), (), s32[]{:S(2)}) async-start(), calls=%async_computation.4 | async-start | bytes 58720256 | tf_op jit(solution)/shard_map/psum | solution.py:28
  857.6 1409.8 %all-reduce.9.cloned.1.call-start = ((), (), s32[]{:S(2)}) async-start(), calls=%async_computation.5 | async-start | bytes 58720256 | tf_op jit(solution)/shard_map/psum | solution.py:28
  1623.5 1436.0 %all-reduce.11.cloned.1.call-start = ((), (), s32[]{:S(2)}) async-start(), calls=%async_computation.6 | async-start | bytes 58720256 | tf_op jit(solution)/shard_map/psum | solution.py:28
  2415.6 1409.8 %all-reduce.13.cloned.1.call-start = ((), (), s32[]{:S(2)}) async-start(), calls=%async_computation.7 | async-start | bytes 58720256 | tf_op jit(solution)/shard_map/psum | solution.py:28
  3181.6 1436.0 %all-reduce.15.cloned.1.call-start = ((), (), s32[]{:S(2)}) async-start(), calls=%async_computation.8 | async-start | bytes 58720256 | tf_op jit(solution)/shard_map/psum | solution.py:28
  3973.8 1409.6 %all-reduce.17.cloned.1.call-start = ((), (), s32[]{:S(2)}) async-start(), calls=%async_computation.9 | async-start | bytes 58720256 | tf_op jit(solution)/shard_map/psum | solution.py:28
Sparse Core Ops, SparseCore 0:
  324.2 159.1 all-gather.2
  636.9 159.1 all-gather.4
  857.7 643.7 all-reduce.6
  1623.6 643.6 all-reduce.8
  2415.8 643.6 all-reduce.10
  3181.7 643.6 all-reduce.12
  3973.9 643.6 all-reduce.14
  4739.6 643.7 all-reduce.16
where the time goes:
time: 5420 us
  waiting for transfers between devices  4240 us (78%)
  matrix products  726 us (13%)
  blocking collectives  240 us (4%)
  other arithmetic  116 us (2%)
  local copies, waits for them, and re-layouts  71.8 us (1%)
    psum x6, waiting for transfers between devices, device_step(): part_sum = lax.psum(part_sum, 'tp')  3860 us
    dot_general x6, matrix products, device_step(): jnp.dot(hidden, full_up[layer], preferred_element_type=jnp.float32)  412 us
    dot_general x6, matrix products, device_step(): jnp.dot(act_up, full_down[layer], preferred_element_type=jnp.float32)  314 us
    ppermute x1, waiting for transfers between devices, device_step(): lax.ppermute(new_up[0].astype(jnp.bfloat16), 'side', perm=[(0, 1)])  137 us
    ppermute x1, waiting for transfers between devices, device_step(): lax.ppermute(new_down[0].astype(jnp.bfloat16), 'side', perm=[(0, 1)])  136 us
    all_to_all x1, blocking collectives, device_step(): band_up = lax.all_to_all(recv_up, 'tp', 2, 1, tiled=True)  121 us
    all_to_all x1, blocking collectives, device_step(): band_down = lax.all_to_all(recv_down, 'tp', 1, 2, tiled=True)  119 us
  transfers between devices with their start and end apart: 10, of which 9 were waited for; matrix products, arithmetic and copies ran while one was open for 2% of the time, Pallas kernels for 0%

commit v1 on v0

v1 whole, which is shorter than its diff:
```python
import jax
import jax.numpy as jnp
from jax import lax
from jax.sharding import PartitionSpec as P


def solution(mesh):
    up_spec = P("side", None, ("rep", "tp"), None)
    down_spec = P("side", None, None, ("rep", "tp"))
    tok_spec = P("side", "rep", None, None)

    def device_step(w_up, w_down, g_up, g_down, learn_rate, prompts):
        is_trainer = lax.axis_index("side") == 0
        rate = learn_rate[0]
        new_up = jnp.where(is_trainer, w_up - rate * g_up, 0.0)
        new_down = jnp.where(is_trainer, w_down - rate * g_down, 0.0)
        layers = w_up.shape[1]
        full_up, full_down = [], []
        for layer in range(layers):
            up_band = (w_up[0, layer] - rate * g_up[0, layer]).astype(jnp.bfloat16)
            down_band = (w_down[0, layer] - rate * g_down[0, layer]).astype(jnp.bfloat16).T
            recv_up = lax.ppermute(up_band, "side", perm=[(0, 1)])
            recv_down = lax.ppermute(down_band, "side", perm=[(0, 1)])
            full_up.append(lax.all_gather(recv_up, ("rep", "tp"), axis=0, tiled=True))
            full_down.append(lax.all_gather(recv_down, ("rep", "tp"), axis=0, tiled=True))
        rows = prompts.shape[2] // mesh.shape["tp"]
        hidden = lax.dynamic_slice_in_dim(prompts[0, 0], lax.axis_index("tp") * rows, rows, 0)
        for layer in range(layers):
            pre_act = jnp.dot(hidden, full_up[layer], preferred_element_type=jnp.float32)
            act_up = jax.nn.gelu(pre_act, approximate=True).astype(jnp.bfloat16)
            part_sum = lax.dot_general(
                act_up, full_down[layer], (((1,), (1,)), ((), ())), preferred_element_type=jnp.float32
            )
            hidden = (hidden.astype(jnp.float32) + part_sum).astype(jnp.bfloat16)
        hidden = lax.all_gather(hidden, "tp", axis=0, tiled=True)
        gen_out = jnp.where(is_trainer, jnp.zeros_like(hidden), hidden)
        return new_up, new_down, gen_out[None, None]

    return jax.shard_map(
        device_step,
        mesh=mesh,
        in_specs=(up_spec, down_spec, up_spec, down_spec, P("side"), tok_spec),
        out_specs=(up_spec, down_spec, tok_spec),
        check_vma=False,
    )
```

time: 5420 us -> 1180 us (0.22)
  waiting for transfers between devices: 4240 us -> 380 us
  blocking collectives: 240 us -> 0 us
  matrix products: 726 us -> 650 us
  local copies, waits for them, and re-layouts: 71.8 us -> 6.29 us
  other arithmetic: 116 us -> 53.3 us
    psum x6 -> x0, waiting for transfers between devices: 3860 us -> none  [device_step(): part_sum = lax.psum(part_sum, 'tp')]
    all_to_all x2 -> x0, blocking collectives: 240 us -> none  [the longest x1 121 us: device_step(): band_up = lax.all_to_all(recv_up, 'tp', 2, 1, tiled=True)]
    convert_element_type x4 -> x1, other arithmetic: 86.6 us -> 10.9 us  [device_step(): up_band = (w_up[0, layer] - rate * g_up[0, layer]).astype(jnp.bfloat16)]
    dot_general x6, matrix products: 412 us -> 353 us  [device_step(): jnp.dot(hidden, full_up[layer], preferred_element_type=jnp.float32)]
    all_gather x2 -> x13, waiting for transfers between devices: 99 us -> 149 us  [the longest x1 149 us: device_step(): hidden = lax.all_gather(hidden, 'tp', axis=0, tiled=True)]
    ppermute x2 -> x12, waiting for transfers between devices: 273 us -> 231 us  [the longest x6 119 us: device_step(): recv_up = lax.ppermute(up_band, 'side', perm=[(0, 1)])]
  transfers between devices with their start and end apart: 10 -> 25, of which waited for: 9 -> 13; matrix products, arithmetic and copies ran while one was open for 2% -> 55% of each run, Pallas kernels for 0% -> 0%
where the time goes in v1:
time: 1180 us; the launch traced here: 1170 us
  matrix products  650 us (55%)
  waiting for transfers between devices  380 us (32%)
  starting transfers between devices  63.1 us (5%)
  other arithmetic  53.3 us (5%)
  between operations  14.9 us (1%)
    dot_general x6, matrix products, device_step(): jnp.dot(hidden, full_up[layer], preferred_element_type=jnp.float32)  353 us
    dot_general x6, matrix products, device_step(): lax.dot_general(act_up, full_down[layer], (((1,), (1,)), ((), ())), prefe...  297 us
    all_gather x1, waiting for transfers between devices, device_step(): hidden = lax.all_gather(hidden, 'tp', axis=0, tiled=True)  149 us
    ppermute x6, waiting for transfers between devices, device_step(): recv_up = lax.ppermute(up_band, 'side', perm=[(0, 1)])  119 us
    ppermute x6, waiting for transfers between devices, device_step(): recv_down = lax.ppermute(down_band, 'side', perm=[(0, 1)])  112 us
    ppermute x6, starting transfers between devices, device_step(): recv_up = lax.ppermute(up_band, 'side', perm=[(0, 1)])  31.4 us
    ppermute x6, starting transfers between devices, device_step(): recv_down = lax.ppermute(down_band, 'side', perm=[(0, 1)])  30.7 us
  transfers between devices with their start and end apart: 25, of which 13 were waited for; matrix products, arithmetic and copies ran while one was open for 55% of the time, Pallas kernels for 0%

profile of v1, /device:TPU:0, one launch (start us, length us, event | category | flops | bytes accessed | tf_op | source)
XLA Modules:
  0.0 1167.0 jit_solution(933276624482695895)
XLA Ops:
  7.2 0.0 all-gather.14.cloned.1.call-start
  7.9 10.9 fusion.67
  18.7 5.2 collective-permute-start
  24.0 23.2 %collective-permute-done = bf16[112,4864]{1,0:T(8,128)(2,1)S(1)} collective-permute-done((bf16[112,4864]{1,0:T(8,128)(2,1)S(1)}, bf16[112,4864]{1,0:T(8,128)(2,1)S(1)}, u32[]{:S(2)}, u32[]{:S(2)}) %collective-permute-start) | collective-permute-done | bytes 1089568 | tf_op jit(solution)/shard_map/ppermute | solution.py:22
  47.2 1.0 copy-done
  48.2 0.0 all-gather.16.cloned.1.call-start
  48.3 11.2 fusion.68
  59.5 5.4 collective-permute-start.1
  64.9 21.4 %collective-permute-done.1 = bf16[112,4864]{1,0:T(8,128)(2,1)} collective-permute-done((bf16[112,4864]{1,0:T(8,128)(2,1)S(1)}, bf16[112,4864]{1,0:T(8,128)(2,1)}, u32[]{:S(2)}, u32[]{:S(2)}) %collective-permute-start.1) | collective-permute-done | bytes 1089568 | tf_op jit(solution)/shard_map/ppermute | solution.py:23
  86.3 0.0 all-gather.16.cloned.1.call-update
  86.3 0.0 all-gather.18.cloned.1.call-start
  86.4 5.4 collective-permute-start.2
  91.8 20.6 %collective-permute-done.2 = bf16[112,4864]{1,0:T(8,128)(2,1)} collective-permute-done((bf16[112,4864]{1,0:T(8,128)(2,1)}, bf16[112,4864]{1,0:T(8,128)(2,1)}, u32[]{:S(2)}, u32[]{:S(2)}) %collective-permute-start.2) | collective-permute-done | bytes 1089568 | tf_op jit(solution)/shard_map/ppermute | solution.py:22
  112.5 0.0 all-gather.18.cloned.1.call-update
  112.5 0.0 all-gather.20.cloned.1.call-start
  112.5 5.5 collective-permute-start.3
  118.0 19.9 %collective-permute-done.3 = bf16[112,4864]{1,0:T(8,128)(2,1)} collective-permute-done((bf16[112,4864]{1,0:T(8,128)(2,1)}, bf16[112,4864]{1,0:T(8,128)(2,1)}, u32[]{:S(2)}, u32[]{:S(2)}) %collective-permute-start.3) | collective-permute-done | bytes 1089568 | tf_op jit(solution)/shard_map/ppermute | solution.py:23
  137.9 0.0 all-gather.22.cloned.1.call-start
  137.9 5.4 collective-permute-start.4
  143.3 19.2 %collective-permute-done.4 = bf16[112,4864]{1,0:T(8,128)(2,1)} collective-permute-done((bf16[112,4864]{1,0:T(8,128)(2,1)}, bf16[112,4864]{1,0:T(8,128)(2,1)}, u32[]{:S(2)}, u32[]{:S(2)}) %collective-permute-start.4) | collective-permute-done | bytes 1089568 | tf_op jit(solution)/shard_map/ppermute | solution.py:22
  162.5 0.0 all-gather.24.cloned.1.call-start
  162.6 5.4 collective-permute-start.5
  168.0 18.6 %collective-permute-done.5 = bf16[112,4864]{1,0:T(8,128)(2,1)} collective-permute-done((bf16[112,4864]{1,0:T(8,128)(2,1)}, bf16[112,4864]{1,0:T(8,128)(2,1)}, u32[]{:S(2)}, u32[]{:S(2)}) %collective-permute-start.5) | collective-permute-done | bytes 1089568 | tf_op jit(solution)/shard_map/ppermute | solution.py:23
  186.6 0.0 all-gather.26.cloned.1.call-start
  186.7 5.4 collective-permute-start.6
  192.1 18.6 %collective-permute-done.6 = bf16[112,4864]{1,0:T(8,128)(2,1)} collective-permute-done((bf16[112,4864]{1,0:T(8,128)(2,1)}, bf16[112,4864]{1,0:T(8,128)(2,1)}, u32[]{:S(2)}, u32[]{:S(2)}) %collective-permute-start.6) | collective-permute-done | bytes 1089568 | tf_op jit(solution)/shard_map/ppermute | solution.py:22
  210.7 0.0 all-gather.28.cloned.1.call-start
  210.8 5.4 collective-permute-start.7
  216.2 18.6 %collective-permute-done.7 = bf16[112,4864]{1,0:T(8,128)(2,1)} collective-permute-done((bf16[112,4864]{1,0:T(8,128)(2,1)}, bf16[112,4864]{1,0:T(8,128)(2,1)}, u32[]{:S(2)}, u32[]{:S(2)}) %collective-permute-start.7) | collective-permute-done | bytes 1089568 | tf_op jit(solution)/shard_map/ppermute | solution.py:23
  234.8 0.0 all-gather.30.cloned.1.call-start
  234.9 5.5 collective-permute-start.8
  240.3 18.6 %collective-permute-done.8 = bf16[112,4864]{1,0:T(8,128)(2,1)} collective-permute-done((bf16[112,4864]{1,0:T(8,128)(2,1)S(1)}, bf16[112,4864]{1,0:T(8,128)(2,1)}, u32[]{:S(2)}, u32[]{:S(2)}) %collective-permute-start.8) | collective-permute-done | bytes 1089568 | tf_op jit(solution)/shard_map/ppermute | solution.py:22
  258.9 0.0 all-gather.32.cloned.1.call-start
  259.0 4.5 collective-permute-start.9
  263.4 18.7 %collective-permute-done.9 = bf16[112,4864]{1,0:T(8,128)(2,1)S(1)} collective-permute-done((bf16[112,4864]{1,0:T(8,128)(2,1)}, bf16[112,4864]{1,0:T(8,128)(2,1)S(1)}, u32[]{:S(2)}, u32[]{:S(2)}) %collective-permute-start.9) | collective-permute-done | bytes 1089568 | tf_op jit(solution)/shard_map/ppermute | solution.py:23
  282.1 1.0 copy-done.1
  283.1 0.0 all-gather.34.cloned.1.call-start
  283.2 4.5 collective-permute-start.10
  287.6 18.6 %collective-permute-done.10 = bf16[112,4864]{1,0:T(8,128)(2,1)S(1)} collective-permute-done((bf16[112,4864]{1,0:T(8,128)(2,1)S(1)}, bf16[112,4864]{1,0:T(8,128)(2,1)S(1)}, u32[]{:S(2)}, u32[]{:S(2)}) %collective-permute-start.10) | collective-permute-done | bytes 1089568 | tf_op jit(solution)/shard_map/ppermute | solution.py:22
  306.2 1.0 copy-done.2
  307.2 0.0 all-gather.36.cloned.1.call-start
  307.3 4.5 collective-permute-start.11
  311.7 14.7 %collective-permute-done.11 = bf16[112,4864]{1,0:T(8,128)(2,1)S(1)} collective-permute-done((bf16[112,4864]{1,0:T(8,128)(2,1)S(1)}, bf16[112,4864]{1,0:T(8,128)(2,1)S(1)}, u32[]{:S(2)}, u32[]{:S(2)}) %collective-permute-start.11) | collective-permute-done | bytes 1089568 | tf_op jit(solution)/shard_map/ppermute | solution.py:23
  326.5 1.0 copy-done.3
  327.5 0.6 all-gather.38.cloned.1.call-start
  328.1 0.0 all-gather.14.cloned.1.call-done
  328.1 58.9 %fusion.7.clone.4 = bf16[4096,4864]{1,0:T(8,128)(2,1)} fusion(bf16[896,4864]{1,0:T(8,128)(2,1)} %all-gather.14.cloned.1.call-done, bf16[1,1,8192,896]{3,2,1,0:T(8,128)(2,1)} %param.11, s32[]{:T(128)S(6)} %select_n.32), kind=kOutput, calls=%fused_computation.13.clone.clone.clone.1 | convolution fusion | flops 35881222144 | bytes 55902212 | tf_op jit(solution)/shard_map/dot_general | solution.py:29
  387.0 49.5 %add_convert_fusion.5 = bf16[4096,896]{1,0:T(8,128)(2,1)} fusion(bf16[896,4864]{1,0:T(8,128)(2,1)} %all-gather.16.cloned.1.call-done, bf16[1,1,8192,896]{3,2,1,0:T(8,128)(2,1)} %param.11, s32[]{:T(128)S(6)} %select_n.32, bf16[4096,4864]{1,0:T(8,128)(2,1)} %fusion.7.clone.4), kind=kOutput, calls=%fused_computation.60 | convolution fusion | flops 35712925696 | bytes 63242244 | tf_op jit(solution)/shard_map/dot_general | solution.py:31
  436.4 58.9 %fusion.15.clone.4 = bf16[4096,4864]{1,0:T(8,128)(2,1)} fusion(bf16[4096,896]{1,0:T(8,128)(2,1)} %add_convert_fusion.5, bf16[896,4864]{1,0:T(8,128)(2,1)} %all-gather.18.cloned.1.call-done), kind=kOutput, calls=%fused_computation.21.clone.clone.clone.clone.clone | convolution fusion | flops 35881222144 | bytes 55902208 | tf_op jit(solution)/shard_map/dot_general | solution.py:29
  495.3 49.6 %add_convert_fusion.4 = bf16[4096,896]{1,0:T(8,128)(2,1)} fusion(bf16[4096,896]{1,0:T(8,128)(2,1)} %add_convert_fusion.5, bf16[896,4864]{1,0:T(8,128)(2,1)} %all-gather.20.cloned.1.call-done, bf16[4096,4864]{1,0:T(8,128)(2,1)} %fusion.15.clone.4), kind=kOutput, calls=%fused_computation.59 | convolution fusion | flops 35712925696 | bytes 63242240 | tf_op jit(solution)/shard_map/dot_general | solution.py:31
  544.9 58.8 %fusion.23.clone.4 = bf16[4096,4864]{1,0:T(8,128)(2,1)} fusion(bf16[4096,896]{1,0:T(8,128)(2,1)} %add_convert_fusion.4, bf16[896,4864]{1,0:T(8,128)(2,1)} %all-gather.22.cloned.1.call-done), kind=kOutput, calls=%fused_computation.29.clone.clone.clone.clone.clone | convolution fusion | flops 35881222144 | bytes 55902208 | tf_op jit(solution)/shard_map/dot_general | solution.py:29
  603.7 49.3 %add_convert_fusion.3 = bf16[4096,896]{1,0:T(8,128)(2,1)} fusion(bf16[4096,896]{1,0:T(8,128)(2,1)} %add_convert_fusion.4, bf16[896,4864]{1,0:T(8,128)(2,1)} %all-gather.24.cloned.1.call-done, bf16[4096,4864]{1,0:T(8,128)(2,1)} %fusion.23.clone.4), kind=kOutput, calls=%fused_computation.58 | convolution fusion | flops 35712925696 | bytes 63242240 | tf_op jit(solution)/shard_map/dot_general | solution.py:31
  653.0 58.8 %fusion.31.clone.4 = bf16[4096,4864]{1,0:T(8,128)(2,1)} fusion(bf16[4096,896]{1,0:T(8,128)(2,1)} %add_convert_fusion.3, bf16[896,4864]{1,0:T(8,128)(2,1)} %all-gather.26.cloned.1.call-done), kind=kOutput, calls=%fused_computation.37.clone.clone.clone.clone.clone | convolution fusion | flops 35881222144 | bytes 55902208 | tf_op jit(solution)/shard_map/dot_general | solution.py:29
  711.9 49.6 %add_convert_fusion.2 = bf16[4096,896]{1,0:T(8,128)(2,1)} fusion(bf16[4096,896]{1,0:T(8,128)(2,1)} %add_convert_fusion.3, bf16[896,4864]{1,0:T(8,128)(2,1)} %all-gather.28.cloned.1.call-done, bf16[4096,4864]{1,0:T(8,128)(2,1)} %fusion.31.clone.4), kind=kOutput, calls=%fused_computation.57 | convolution fusion | flops 35712925696 | bytes 63242240 | tf_op jit(solution)/shard_map/dot_general | solution.py:31
  761.4 58.8 %fusion.39.clone.4 = bf16[4096,4864]{1,0:T(8,128)(2,1)} fusion(bf16[4096,896]{1,0:T(8,128)(2,1)} %add_convert_fusion.2, bf16[896,4864]{1,0:T(8,128)(2,1)} %all-gather.30.cloned.1.call-done), kind=kOutput, calls=%fused_computation.45.clone.clone.clone.clone.clone | convolution fusion | flops 35881222144 | bytes 55902208 | tf_op jit(solution)/shard_map/dot_general | solution.py:29
  820.3 49.3 %add_convert_fusion.1 = bf16[4096,896]{1,0:T(8,128)(2,1)} fusion(bf16[4096,896]{1,0:T(8,128)(2,1)} %add_convert_fusion.2, bf16[896,4864]{1,0:T(8,128)(2,1)} %all-gather.32.cloned.1.call-done, bf16[4096,4864]{1,0:T(8,128)(2,1)} %fusion.39.clone.4), kind=kOutput, calls=%fused_computation.56 | convolution fusion | flops 35712925696 | bytes 63242240 | tf_op jit(solution)/shard_map/dot_general | solution.py:31
  869.6 58.8 %fusion.47.clone.6 = bf16[4096,4864]{1,0:T(8,128)(2,1)} fusion(bf16[4096,896]{1,0:T(8,128)(2,1)} %add_convert_fusion.1, bf16[896,4864]{1,0:T(8,128)(2,1)} %all-gather.34.cloned.1.call-done), kind=kOutput, calls=%fused_computation.53.clone.clone.clone.clone.clone.1 | convolution fusion | flops 35881222144 | bytes 55902208 | tf_op jit(solution)/shard_map/dot_general | solution.py:29
  928.4 49.4 %add_convert_fusion = bf16[4096,896]{1,0:T(8,128)(2,1)} fusion(bf16[4096,896]{1,0:T(8,128)(2,1)} %add_convert_fusion.1, bf16[896,4864]{1,0:T(8,128)(2,1)} %all-gather.36.cloned.1.call-done, bf16[4096,4864]{1,0:T(8,128)(2,1)} %fusion.47.clone.6), kind=kOutput, calls=%fused_computation.55 | convolution fusion | flops 35712925696 | bytes 63242240 | tf_op jit(solution)/shard_map/dot_general | solution.py:31
  977.9 14.7 %subtract_select_fusion = f32[1,6,4864,112]{2,3,1,0:T(8,128)} fusion(f32[1,6,4864,112]{2,3,1,0:T(8,128)} %param.7, f32[1,6,4864,112]{2,3,1,0:T(8,128)} %param.9, f32[]{:T(128)} %bitcast.89, pred[]{:T(512)S(6)} %eq.3), kind=kLoop, calls=%fused_computation.61 | loop fusion | flops 9805824 | bytes 39223300 | tf_op jit(solution)/shard_map/jit(_where)/select_n | solution.py:16
  992.5 1.1 slice-done.2
  993.7 1.2 slice-done.3
  994.9 10.7 subtract_select_fusion.1
  1005.5 148.9 %all-gather.38.cloned.1.call-done = bf16[8192,896]{1,0:T(8,128)(2,1)} async-done(((bf16[4096,896]{1,0:T(8,128)(2,1)}), bf16[8192,896]{1,0:T(8,128)(2,1)}) %all-gather.38.cloned.1.call-update) | async-done | bytes 14680080 | tf_op jit(solution)/shard_map/all_gather | solution.py:35
  1154.4 5.8 select_bitcast_fusion
  (33 shorter events, 0.2 us)
Async XLA Ops:
  7.2 320.9 %all-gather.14.cloned.1.call-start = ((), (), s32[]{:S(2)}) async-start(), calls=%async_computation | async-start | bytes 9805824 | tf_op jit(solution)/shard_map/all_gather | solution.py:24
  18.7 28.4 %collective-permute-start = (bf16[112,4864]{1,0:T(8,128)(2,1)S(1)}, bf16[112,4864]{1,0:T(8,128)(2,1)S(1)}, u32[]{:S(2)}, u32[]{:S(2)}) collective-permute-start(bf16[112,4864]{1,0:T(8,128)(2,1)S(1)} %get-tuple-element.7), channel_id=1, source_target_pairs={{0,4},{1,5},{2,6},{3,7},{8,12},{9,13},{10,14},{11,15}} | collective-permute-start | bytes 3268616 | tf_op jit(solution)/shard_map/ppermute | solution.py:22
  47.2 1.0 copy-start
  48.2 338.8 %all-gather.16.cloned.1.call-start = ((), (), s32[]{:S(2)}) async-start(), calls=%async_computation.1 | async-start | bytes 9805824 | tf_op jit(solution)/shard_map/all_gather | solution.py:25
  59.5 26.8 %collective-permute-start.1 = (bf16[112,4864]{1,0:T(8,128)(2,1)S(1)}, bf16[112,4864]{1,0:T(8,128)(2,1)}, u32[]{:S(2)}, u32[]{:S(2)}) collective-permute-start(bf16[112,4864]{1,0:T(8,128)(2,1)S(1)} %get-tuple-element.13), channel_id=1, source_target_pairs={{0,4},{1,5},{2,6},{3,7},{8,12},{9,13},{10,14},{11,15}} | collective-permute-start | bytes 3268616 | tf_op jit(solution)/shard_map/ppermute | solution.py:23
  86.3 350.1 %all-gather.18.cloned.1.call-start = ((), (), s32[]{:S(2)}) async-start(), calls=%async_computation.2 | async-start | bytes 9805824 | tf_op jit(solution)/shard_map/all_gather | solution.py:24
  86.4 26.1 %collective-permute-start.2 = (bf16[112,4864]{1,0:T(8,128)(2,1)}, bf16[112,4864]{1,0:T(8,128)(2,1)}, u32[]{:S(2)}, u32[]{:S(2)}) collective-permute-start(bf16[112,4864]{1,0:T(8,128)(2,1)} %get-tuple-element.6), channel_id=1, source_target_pairs={{0,4},{1,5},{2,6},{3,7},{8,12},{9,13},{10,14},{11,15}} | collective-permute-start | bytes 3268616 | tf_op jit(solution)/shard_map/ppermute | solution.py:22
  112.5 382.8 %all-gather.20.cloned.1.call-start = ((), (), s32[]{:S(2)}) async-start(), calls=%async_computation.3 | async-start | bytes 9805824 | tf_op jit(solution)/shard_map/all_gather | solution.py:25
  112.5 25.3 %collective-permute-start.3 = (bf16[112,4864]{1,0:T(8,128)(2,1)}, bf16[112,4864]{1,0:T(8,128)(2,1)}, u32[]{:S(2)}, u32[]{:S(2)}) collective-permute-start(bf16[112,4864]{1,0:T(8,128)(2,1)} %get-tuple-element.12), channel_id=1, source_target_pairs={{0,4},{1,5},{2,6},{3,7},{8,12},{9,13},{10,14},{11,15}} | collective-permute-start | bytes 3268616 | tf_op jit(solution)/shard_map/ppermute | solution.py:23
  137.9 407.0 %all-gather.22.cloned.1.call-start = ((), (), s32[]{:S(2)}) async-start(), calls=%async_computation.4 | async-start | bytes 9805824 | tf_op jit(solution)/shard_map/all_gather | solution.py:24
  137.9 24.6 %collective-permute-start.4 = (bf16[112,4864]{1,0:T(8,128)(2,1)}, bf16[112,4864]{1,0:T(8,128)(2,1)}, u32[]{:S(2)}, u32[]{:S(2)}) collective-permute-start(bf16[112,4864]{1,0:T(8,128)(2,1)} %get-tuple-element.5), channel_id=1, source_target_pairs={{0,4},{1,5},{2,6},{3,7},{8,12},{9,13},{10,14},{11,15}} | collective-permute-start | bytes 3268616 | tf_op jit(solution)/shard_map/ppermute | solution.py:22
  162.5 441.2 %all-gather.24.cloned.1.call-start = ((), (), s32[]{:S(2)}) async-start(), calls=%async_computation.5 | async-start | bytes 9805824 | tf_op jit(solution)/shard_map/all_gather | solution.py:25
  162.6 24.0 %collective-permute-start.5 = (bf16[112,4864]{1,0:T(8,128)(2,1)}, bf16[112,4864]{1,0:T(8,128)(2,1)}, u32[]{:S(2)}, u32[]{:S(2)}) collective-permute-start(bf16[112,4864]{1,0:T(8,128)(2,1)} %get-tuple-element.11), channel_id=1, source_target_pairs={{0,4},{1,5},{2,6},{3,7},{8,12},{9,13},{10,14},{11,15}} | collective-permute-start | bytes 3268616 | tf_op jit(solution)/shard_map/ppermute | solution.py:23
  186.6 466.4 %all-gather.26.cloned.1.call-start = ((), (), s32[]{:S(2)}) async-start(), calls=%async_computation.6 | async-start | bytes 9805824 | tf_op jit(solution)/shard_map/all_gather | solution.py:24
  186.7 24.0 %collective-permute-start.6 = (bf16[112,4864]{1,0:T(8,128)(2,1)}, bf16[112,4864]{1,0:T(8,128)(2,1)}, u32[]{:S(2)}, u32[]{:S(2)}) collective-permute-start(bf16[112,4864]{1,0:T(8,128)(2,1)} %get-tuple-element.4), channel_id=1, source_target_pairs={{0,4},{1,5},{2,6},{3,7},{8,12},{9,13},{10,14},{11,15}} | collective-permute-start | bytes 3268616 | tf_op jit(solution)/shard_map/ppermute | solution.py:22
  210.7 501.2 %all-gather.28.cloned.1.call-start = ((), (), s32[]{:S(2)}) async-start(), calls=%async_computation.7 | async-start | bytes 9805824 | tf_op jit(solution)/shard_map/all_gather | solution.py:25
  210.8 24.0 %collective-permute-start.7 = (bf16[112,4864]{1,0:T(8,128)(2,1)}, bf16[112,4864]{1,0:T(8,128)(2,1)}, u32[]{:S(2)}, u32[]{:S(2)}) collective-permute-start(bf16[112,4864]{1,0:T(8,128)(2,1)} %get-tuple-element.10), channel_id=1, source_target_pairs={{0,4},{1,5},{2,6},{3,7},{8,12},{9,13},{10,14},{11,15}} | collective-permute-start | bytes 3268616 | tf_op jit(solution)/shard_map/ppermute | solution.py:23
  234.8 526.6 %all-gather.30.cloned.1.call-start = ((), (), s32[]{:S(2)}) async-start(), calls=%async_computation.8 | async-start | bytes 9805824 | tf_op jit(solution)/shard_map/all_gather | solution.py:24
  234.9 24.0 %collective-permute-start.8 = (bf16[112,4864]{1,0:T(8,128)(2,1)S(1)}, bf16[112,4864]{1,0:T(8,128)(2,1)}, u32[]{:S(2)}, u32[]{:S(2)}) collective-permute-start(bf16[112,4864]{1,0:T(8,128)(2,1)S(1)} %get-tuple-element.8), channel_id=1, source_target_pairs={{0,4},{1,5},{2,6},{3,7},{8,12},{9,13},{10,14},{11,15}} | collective-permute-start | bytes 3268616 | tf_op jit(solution)/shard_map/ppermute | solution.py:22
  258.9 561.4 %all-gather.32.cloned.1.call-start = ((), (), s32[]{:S(2)}) async-start(), calls=%async_computation.9 | async-start | bytes 9805824 | tf_op jit(solution)/shard_map/all_gather | solution.py:25
  259.0 23.1 %collective-permute-start.9 = (bf16[112,4864]{1,0:T(8,128)(2,1)}, bf16[112,4864]{1,0:T(8,128)(2,1)S(1)}, u32[]{:S(2)}, u32[]{:S(2)}) collective-permute-start(bf16[112,4864]{1,0:T(8,128)(2,1)} %get-tuple-element.14), channel_id=1, source_target_pairs={{0,4},{1,5},{2,6},{3,7},{8,12},{9,13},{10,14},{11,15}} | collective-permute-start | bytes 3268616 | tf_op jit(solution)/shard_map/ppermute | solution.py:23
  282.1 1.0 copy-start.1
  283.1 586.5 %all-gather.34.cloned.1.call-start = ((), (), s32[]{:S(2)}) async-start(), calls=%async_computation.10 | async-start | bytes 9805824 | tf_op jit(solution)/shard_map/all_gather | solution.py:24
  283.2 23.0 %collective-permute-start.10 = (bf16[112,4864]{1,0:T(8,128)(2,1)S(1)}, bf16[112,4864]{1,0:T(8,128)(2,1)S(1)}, u32[]{:S(2)}, u32[]{:S(2)}) collective-permute-start(bf16[112,4864]{1,0:T(8,128)(2,1)S(1)} %get-tuple-element.3), channel_id=1, source_target_pairs={{0,4},{1,5},{2,6},{3,7},{8,12},{9,13},{10,14},{11,15}} | collective-permute-start | bytes 3268616 | tf_op jit(solution)/shard_map/ppermute | solution.py:22
  306.2 1.0 copy-start.2
  307.2 621.2 %all-gather.36.cloned.1.call-start = ((), (), s32[]{:S(2)}) async-start(), calls=%async_computation.11 | async-start | bytes 9805824 | tf_op jit(solution)/shard_map/all_gather | solution.py:25
  307.3 19.2 %collective-permute-start.11 = (bf16[112,4864]{1,0:T(8,128)(2,1)S(1)}, bf16[112,4864]{1,0:T(8,128)(2,1)S(1)}, u32[]{:S(2)}, u32[]{:S(2)}) collective-permute-start(bf16[112,4864]{1,0:T(8,128)(2,1)S(1)} %get-tuple-element.9), channel_id=1, source_target_pairs={{0,4},{1,5},{2,6},{3,7},{8,12},{9,13},{10,14},{11,15}} | collective-permute-start | bytes 3268616 | tf_op jit(solution)/shard_map/ppermute | solution.py:23
  326.5 1.0 copy-start.3
  327.5 827.0 %all-gather.38.cloned.1.call-start = ((), (), s32[]{:S(2)}) async-start(), calls=%async_computation.12 | async-start | bytes 22020096 | tf_op jit(solution)/shard_map/all_gather | solution.py:35
  977.8 14.7 %slice-start = ((s8[13074432]{0:T(1024)(128)(4,1)}), s8[491520]{0:T(1024)(128)(4,1)S(1)}, s32[]{:S(2)}) async-start(s8[13074432]{0:T(1024)(128)(4,1)} %bitcast.92), calls=%async_computation.13 | async-start | bytes 983040
  977.8 14.7 %slice-start.1 = ((s8[13074432]{0:T(1024)(128)(4,1)}), s8[4194304]{0:T(1024)(128)(4,1)S(1)}, s32[]{:S(2)}) async-start(s8[13074432]{0:T(1024)(128)(4,1)} %bitcast.92), calls=%async_computation.14 | async-start | bytes 8388608
  977.8 15.8 %slice-start.2 = ((s8[13074432]{0:T(1024)(128)(4,1)}), s8[4194304]{0:T(1024)(128)(4,1)S(1)}, s32[]{:S(2)}) async-start(s8[13074432]{0:T(1024)(128)(4,1)} %bitcast.92), calls=%async_computation.15 | async-start | bytes 8388608
  977.8 17.0 %slice-start.3 = ((s8[13074432]{0:T(1024)(128)(4,1)}), s8[4194304]{0:T(1024)(128)(4,1)S(1)}, s32[]{:S(2)}) async-start(s8[13074432]{0:T(1024)(128)(4,1)} %bitcast.92), calls=%async_computation.16 | async-start | bytes 8388608
Sparse Core Ops, SparseCore 0:
  48.3 53.7 all-gather.13
  104.0 51.6 all-gather.15
  157.6 51.6 all-gather.17
  211.0 51.6 all-gather.19
  264.4 51.6 all-gather.21
  317.8 51.6 all-gather.23
  371.4 51.6 all-gather.25
  425.0 51.6 all-gather.27
  478.5 51.7 all-gather.29
  532.6 51.6 all-gather.31
  586.1 51.6 all-gather.33
  640.1 51.6 all-gather.35
  977.9 176.4 all-gather.37

commit v2 on v0

v2 whole, which is shorter than its diff:
```python
import functools

import jax
import jax.numpy as jnp
from jax import lax
from jax.experimental import pallas as pl
from jax.experimental.pallas import tpu as pltpu
from jax.sharding import PartitionSpec as P

MESH = pl.DeviceIdType.MESH
UNIT = 256
HALF = 2048
OUT_ROWS = 512
LOAD_SLOTS = 4
STAGE_SLOTS = 8
GELU_A = 0.7978845608028654
GELU_B = 0.7978845608028654 * 0.044715


def gelu(a):
    return a * (0.5 * jnp.tanh(a * (GELU_A + GELU_B * (a * a))) + 0.5)


def kernel(
    rate_ref, w_up, w_dn, g_up, g_dn, prompts, out, wbuf,
    h, p, wv, fin, stage, rows_buf, zrow,
    rs, ss, lsem, fsem, tss, iosem, osem,
):
    layers, band, hidden = w_up.shape
    chunks = hidden // UNIT
    total = layers * chunks
    pairs = (chunks - 1) // 2
    n_rows, d = out.shape
    my_rows = n_rows // 2
    halves = my_rows // HALF
    blocks = my_rows // OUT_ROWS

    tp = lax.axis_index("tp")
    side = lax.axis_index("side")
    rep = lax.axis_index("rep")
    x, k = rep // 2, rep % 2
    flip_tp = 1 - tp
    flip_rep = (1 - x) * 2 + k
    sib_rep = x * 2 + (1 - k)

    def band_of(r, t):
        return pl.multiple_of((r * 2 + t) * band, 16)

    own = band_of(rep, tp)
    znb = band_of(rep, flip_tp)
    xnb = band_of(flip_rep, tp)
    dia = band_of(flip_rep, flip_tp)

    def both(c, b):
        return wbuf.at[c, :, pl.ds(b, band), :]

    def one(c, m, b):
        return wbuf.at[c, m, pl.ds(b, band), :]

    Y, YD, Z, X, DG, SB = range(6)

    def send(src, dst, ssem, rsem, t, s, r):
        pltpu.make_async_remote_copy(
            src_ref=src, dst_ref=dst, send_sem=ssem, recv_sem=rsem,
            device_id={"tp": t, "side": s, "rep": r}, device_id_type=MESH,
        ).start()

    def wait(ref, sem):
        pltpu.make_async_copy(ref, ref, sem).wait()

    @pl.when(side == 0)
    def _():
        rate = rate_ref[0]

        def loads(c):
            l, j = c // chunks, c % chunks
            cols = pl.ds(pl.multiple_of(j * UNIT, UNIT), UNIT)
            slot = c % LOAD_SLOTS
            return [
                pltpu.make_async_copy(r.at[l, :, cols], fin.at[slot, i], lsem.at[slot, i])
                for i, r in enumerate((w_up, g_up, w_dn, g_dn))
            ]

        for c in range(LOAD_SLOTS - 1):
            for cp in loads(c):
                cp.start()

        def send_chunk(c):
            slot = c % STAGE_SLOTS
            send(stage.at[slot], both(c, own), tss.at[slot, 0], rs.at[Y, c], tp, 1, rep)
            send(stage.at[slot, 1], one(c, 1, own), tss.at[slot, 1], rs.at[DG, c], flip_tp, 0, flip_rep)

        def wait_sent(c):
            slot = c % STAGE_SLOTS
            wait(stage.at[slot], tss.at[slot, 0])
            wait(stage.at[slot, 1], tss.at[slot, 1])

        def relay(c):
            wait(one(c, 1, dia), rs.at[DG, c])
            send(one(c, 1, dia), one(c, 1, dia), ss.at[0, c // chunks], rs.at[YD, c], tp, 1, rep)

        lag = 3

        def body(c, _):
            @pl.when(c < total)
            def _():
                @pl.when(c + LOAD_SLOTS - 1 < total)
                def _():
                    for cp in loads(c + LOAD_SLOTS - 1):
                        cp.start()

                for cp in loads(c):
                    cp.wait()
                slot, lslot = c % STAGE_SLOTS, c % LOAD_SLOTS

                @pl.when(c >= STAGE_SLOTS)
                def _():
                    wait_sent(c - STAGE_SLOTS)

                stage[slot, 0] = (fin[lslot, 0] - rate * fin[lslot, 1]).astype(jnp.bfloat16)
                stage[slot, 1] = (fin[lslot, 2] - rate * fin[lslot, 3]).astype(jnp.bfloat16)

            @pl.when((c >= 1) & (c < total + 1))
            def _():
                send_chunk(c - 1)

            @pl.when(c >= lag)
            def _():
                relay(c - lag)

            return 0

        lax.fori_loop(0, total + lag, body, 0)

        zrow[...] = jnp.zeros_like(zrow)
        copies = [
            pltpu.make_async_copy(zrow, out.at[pl.ds(b * OUT_ROWS, OUT_ROWS)], iosem.at[b])
            for b in range(2 * blocks)
        ]
        for cp in copies:
            cp.start()

        def drain(c, _):
            wait_sent(total - STAGE_SLOTS + c)
            return 0

        lax.fori_loop(0, STAGE_SLOTS, drain, 0)
        for l in range(layers):
            wait(wbuf.at[pl.ds(l * chunks, chunks), 0, pl.ds(0, band), :], ss.at[0, l])
        for cp in copies:
            cp.wait()

    @pl.when(side == 1)
    def _():
        def y_stage(c):
            l = c // chunks
            wait(both(c, own), rs.at[Y, c])
            send(both(c, own), both(c, own), ss.at[0, l], rs.at[Z, c], flip_tp, 1, rep)
            send(both(c, own), both(c, own), ss.at[1, l], rs.at[X, c], tp, 1, flip_rep)
            send(one(c, 0, own), one(c, 0, own), ss.at[2, l], rs.at[DG, c], flip_tp, 1, flip_rep)
            send(both(c, own), both(c, own), ss.at[3, l], rs.at[SB, c], tp, 1, sib_rep)

        def n_stage(c):
            l = c // chunks
            wait(both(c, znb), rs.at[Z, c])
            send(both(c, znb), both(c, znb), ss.at[4, l], rs.at[SB, c], tp, 1, sib_rep)
            wait(both(c, xnb), rs.at[X, c])
            send(both(c, xnb), both(c, xnb), ss.at[5, l], rs.at[SB, c], tp, 1, sib_rep)
            wait(one(c, 0, dia), rs.at[DG, c])
            send(one(c, 0, dia), one(c, 0, dia), ss.at[6, l], rs.at[SB, c], tp, 1, sib_rep)
            wait(one(c, 1, dia), rs.at[YD, c])
            send(one(c, 1, dia), one(c, 1, dia), ss.at[7, l], rs.at[SB, c], tp, 1, sib_rep)

        def wload(c, slot, half):
            cols = pl.ds(half * UNIT, UNIT)
            return [
                pltpu.make_async_copy(wbuf.at[c, m], wv.at[slot, m, :, cols], fsem.at[slot, half, m])
                for m in range(2)
            ]

        def s_stage(c, slot, half):
            wait(wbuf.at[c, :, pl.ds(0, 4 * band), :], rs.at[SB, c])
            for cp in wload(c, slot, half):
                cp.start()

        def guarded(fn, c, *a):
            @pl.when(c < total)
            def _():
                fn(c, *a)

        base = tp * my_rows

        def pload(b, slot):
            return pltpu.make_async_copy(
                prompts.at[pl.ds(base + b * OUT_ROWS, OUT_ROWS)], rows_buf.at[slot], iosem.at[slot]
            )

        pload(0, 0).start()
        for b in range(blocks):
            if b + 1 < blocks:
                pload(b + 1, (b + 1) % 2).start()
            pload(b, b % 2).wait()
            per = HALF // OUT_ROWS
            h[b // per, :, pl.ds((b % per) * OUT_ROWS, OUT_ROWS)] = rows_buf[b % 2].T

        y_stage(0)
        y_stage(1)
        n_stage(0)
        n_stage(1)
        y_stage(2)
        y_stage(3)
        s_stage(0, 0, 0)
        s_stage(1, 0, 1)
        n_stage(2)
        n_stage(3)
        y_stage(4)
        y_stage(5)

        def compute(slot, width, first):
            def half_body(i, _):
                a = lax.dot_general(
                    wv[slot, 0, :, :width], h[i], (((0,), (0,)), ((), ())), preferred_element_type=jnp.float32
                )
                u = gelu(a).astype(jnp.bfloat16)
                prev = jnp.where(first, 0.0, p[i])
                p[i] = prev + jnp.dot(wv[slot, 1, :, :width], u, preferred_element_type=jnp.float32)
                return 0

            lax.fori_loop(0, halves, half_body, 0)

        def layer_body(l, _):
            c_layer = l * chunks

            def pair_body(i, _):
                step = l * (pairs + 1) + i
                slot = step % 2
                c0 = c_layer + 2 * i
                for half in range(2):
                    for cp in wload(c0 + half, slot, half):
                        cp.wait()
                guarded(y_stage, c0 + 6)
                guarded(y_stage, c0 + 7)
                guarded(n_stage, c0 + 4)
                guarded(n_stage, c0 + 5)
                s_stage(c0 + 2, 1 - slot, 0)

                @pl.when(i < pairs - 1)
                def _():
                    s_stage(c0 + 3, 1 - slot, 1)

                compute(slot, 2 * UNIT, i == 0)
                return 0

            lax.fori_loop(0, pairs, pair_body, 0)
            step = l * (pairs + 1) + pairs
            slot = step % 2
            c0 = c_layer + 2 * pairs
            for cp in wload(c0, slot, 0):
                cp.wait()
            guarded(y_stage, c0 + 6)
            guarded(n_stage, c0 + 4)
            guarded(s_stage, c0 + 1, 1 - slot, 0)
            guarded(s_stage, c0 + 2, 1 - slot, 1)
            compute(slot, UNIT, False)

            @pl.when(l < layers - 1)
            def _():
                def fin_body(b, _):
                    cols = pl.ds(pl.multiple_of((b % 4) * (HALF // 4), HALF // 4), HALF // 4)
                    i = b // 4
                    h[i, :, cols] = (h[i, :, cols].astype(jnp.float32) + p[i, :, cols]).astype(jnp.bfloat16)
                    return 0

                lax.fori_loop(0, halves * 4, fin_body, 0)

            return 0

        lax.fori_loop(0, layers, layer_body, 0)

        per = HALF // OUT_ROWS

        def put(b):
            rows = pl.ds(base + b * OUT_ROWS, OUT_ROWS)
            pltpu.make_async_copy(rows_buf.at[b % 2], out.at[rows], iosem.at[b % 2]).start()
            send(rows_buf.at[b % 2], out.at[rows], tss.at[b % 2, 0], osem.at[b], flip_tp, 1, rep)

        def put_wait(b):
            wait(rows_buf.at[b % 2], iosem.at[b % 2])
            wait(rows_buf.at[b % 2], tss.at[b % 2, 0])

        for b in range(blocks):
            if b >= 2:
                put_wait(b - 2)
            cols = pl.ds((b % per) * OUT_ROWS, OUT_ROWS)
            i = b // per
            rows_buf[b % 2] = (h[i, :, cols].astype(jnp.float32) + p[i, :, cols]).astype(jnp.bfloat16).T
            if b >= 1:
                put(b - 1)
        put(blocks - 1)
        put_wait(blocks - 2)
        put_wait(blocks - 1)
        other = flip_tp * my_rows
        for b in range(blocks):
            wait(out.at[pl.ds(other + b * OUT_ROWS, OUT_ROWS)], osem.at[b])
        kinds = [2, 2, 1, 2, 2, 2, 1, 1]
        for l in range(layers):
            for i, n in enumerate(kinds):
                wait(wbuf.at[pl.ds(l * chunks, chunks), pl.ds(0, n), pl.ds(0, band), :], ss.at[i, l])


def solution(mesh):
    up_spec = P("side", None, ("rep", "tp"), None)
    down_spec = P("side", None, None, ("rep", "tp"))
    tok_spec = P("side", "rep", None, None)

    def device_step(w_up, w_down, g_up, g_down, learn_rate, prompts):
        is_trainer = lax.axis_index("side") == 0
        rate = learn_rate[0]
        layers, band, hidden = w_up.shape[1:]
        n_rows, d = prompts.shape[2:]
        total = layers * hidden // UNIT
        w_dn = jnp.swapaxes(w_down[0], 1, 2)
        g_dn = jnp.swapaxes(g_down[0], 1, 2)
        my_rows = n_rows // 2
        blocks = my_rows // OUT_ROWS
        any_spec = pl.BlockSpec(memory_space=pl.ANY)
        gen_out, _ = pl.pallas_call(
            kernel,
            name="sync_and_forward",
            out_shape=(
                jax.ShapeDtypeStruct((n_rows, d), jnp.bfloat16),
                jax.ShapeDtypeStruct((total, 2, d, UNIT), jnp.bfloat16),
            ),
            in_specs=[pl.BlockSpec(memory_space=pltpu.SMEM)] + [any_spec] * 5,
            out_specs=(any_spec, any_spec),
            scratch_shapes=[
                pltpu.VMEM((my_rows // HALF, d, HALF), jnp.bfloat16),
                pltpu.VMEM((my_rows // HALF, d, HALF), jnp.float32),
                pltpu.VMEM((2, 2, d, 2 * UNIT), jnp.bfloat16),
                pltpu.VMEM((LOAD_SLOTS, 4, band, UNIT), jnp.float32),
                pltpu.VMEM((STAGE_SLOTS, 2, band, UNIT), jnp.bfloat16),
                pltpu.VMEM((2, OUT_ROWS, d), jnp.bfloat16),
                pltpu.VMEM((OUT_ROWS, d), jnp.bfloat16),
                pltpu.SemaphoreType.DMA((6, total)),
                pltpu.SemaphoreType.DMA((8, layers)),
                pltpu.SemaphoreType.DMA((LOAD_SLOTS, 4)),
                pltpu.SemaphoreType.DMA((2, 2, 2)),
                pltpu.SemaphoreType.DMA((STAGE_SLOTS, 2)),
                pltpu.SemaphoreType.DMA((2 * blocks,)),
                pltpu.SemaphoreType.DMA((blocks,)),
            ],
            compiler_params=pltpu.CompilerParams(
                has_side_effects=True, vmem_limit_bytes=60 * 1024 * 1024
            ),
        )(learn_rate, w_up[0], w_dn, g_up[0], g_dn, prompts[0, 0])
        new_up = jnp.where(is_trainer, w_up - rate * g_up, 0.0)
        new_down = jnp.where(is_trainer, w_down - rate * g_down, 0.0)
        return new_up, new_down, gen_out[None, None]

    return jax.shard_map(
        device_step,
        mesh=mesh,
        in_specs=(up_spec, down_spec, up_spec, down_spec, P("side"), tok_spec),
        out_specs=(up_spec, down_spec, tok_spec),
        check_vma=False,
    )
```

time: 5420 us -> 757 us (0.14)
  the two profiles are of different devices: /device:TPU:0 before, /device:TPU:4 now
where the time goes in v2:
time: 757 us
  Pallas kernels  717 us (95%)
  other arithmetic  19.9 us (3%)
  local copies, waits for them, and re-layouts  19.1 us (3%)
    pallas_call x1, Pallas kernels, device_step(): pl.pallas_call(kernel, name='sync_and_forward', out_shape=(jax.ShapeDtype...  717 us
    unnamed x5, local copies, waits for them, and re-layouts  19.1 us

profile of v2, /device:TPU:4, one launch (start us, length us, event | category | flops | bytes accessed | tf_op | source)
XLA Modules:
  0.0 757.2 jit_solution(9795577118098026881)
XLA Ops:
  1.3 0.0 copy-start
  1.3 0.0 copy-start.1
  1.3 14.7 %subtract_select_fusion.1 = f32[1,6,112,4864]{3,2,1,0:T(8,128)} fusion(f32[1,6,112,4864]{3,2,1,0:T(8,128)} %param.6, f32[1,6,112,4864]{3,2,1,0:T(8,128)} %param.8, f32[]{:T(128)} %bitcast.11, pred[]{:T(512)S(6)} %eq.3), kind=kLoop, calls=%fused_computation.1 | loop fusion | flops 9805824 | bytes 39223300 | tf_op jit(solution)/shard_map/jit(_where)/select_n | solution.py:356
  16.0 2.2 copy-done
  18.2 3.7 copy-done.1
  22.0 5.3 subtract_select_fusion
  27.2 716.9 %sync_and_forward.1 = (bf16[8192,896]{1,0:T(8,128)(2,1)}, bf16[114,2,896,256]{3,2,1,0:T(8,128)(2,1)}) custom-call(f32[1]{0:T(128)} %copy.10.rate_ref, f32[6,112,4864]{2,1,0:T(8,128)} %bitcast.13, f32[6,112,4864]{2,1,0:T(8,128)} %bitcast.15, f32[6,112,4864]{2,1,0:T(8,128)} %bitcast.14, f32[6,112,4864]{2,1,0:T(8,128)} %bitcast.16, bf16[8192,896]{1,0:T(8,128)(2,1)} %bitcast.17), custom_call_target="tpu_custom_call" | custom-call | tf_op jit(solution)/shard_map/sync_and_forward/pallas_call | solution.py:327
  744.1 13.1 %copy.11 = bf16[1,1,8192,896]{3,2,1,0:T(8,128)(2,1)} copy(bf16[1,1,8192,896]{3,2,1,0:T(8,128)(2,1)} %bitcast.18) | data formatting | bytes 29360128
Async XLA Ops:
  1.3 16.9 %copy-start = (f32[1,6,4864,112]{2,3,1,0:T(8,128)S(1)}, f32[1,6,4864,112]{2,3,1,0:T(8,128)}, u32[]{:S(2)}) copy-start(f32[1,6,4864,112]{2,3,1,0:T(8,128)} %param.7) | copy-start | bytes 39223300
  1.3 20.7 %copy-start.1 = (f32[1,6,4864,112]{2,3,1,0:T(8,128)S(1)}, f32[1,6,4864,112]{2,3,1,0:T(8,128)}, u32[]{:S(2)}) copy-start(f32[1,6,4864,112]{2,3,1,0:T(8,128)} %param.9) | copy-start | bytes 39223300

commit v3 on v0

v3 whole, which is shorter than its diff:
```python
import jax
import jax.numpy as jnp
from jax import lax
from jax.experimental import pallas as pl
from jax.experimental.pallas import tpu as pltpu
from jax.sharding import PartitionSpec as P

MESH = pl.DeviceIdType.MESH
UNIT = 256
GROUP = 4
BLOCK = 1024
PIECE = 128
LOAD_SLOTS = 4
STAGE_SLOTS = 8
GELU_A = 0.7978845608028654
GELU_B = 0.7978845608028654 * 0.044715


def gelu(a):
    return a * (0.5 * jnp.tanh(a * (GELU_A + GELU_B * (a * a))) + 0.5)


def relays_of(rb, blocks, pieces):
    return pieces // 2 - (rb == blocks - 1).astype(jnp.int32)


def sync_kernel(
    rate_ref, w_up, w_dn, g_up, g_dn, prompts, out, wbuf, rin, rx,
    h, p, wv, fin, stage, rows_buf,
    rs, ss, lsem, fsem, tss, iosem, psem, osem, rsem,
):
    layers, band, hidden = w_up.shape
    chunks = hidden // UNIT
    total = layers * chunks
    groups = -(-chunks // GROUP)
    lead = chunks - (groups - 1) * GROUP
    n_rows, d = out.shape
    my_rows = n_rows // 2
    blocks = my_rows // BLOCK
    pieces = BLOCK // PIECE
    n_relay = blocks * (pieces // 2) - 1

    tp = lax.axis_index("tp")
    side = lax.axis_index("side")
    rep = lax.axis_index("rep")
    x, k = rep // 2, rep % 2
    flip_tp = 1 - tp
    flip_rep = (1 - x) * 2 + k
    sib_rep = x * 2 + (1 - k)

    def band_of(r, t):
        return pl.multiple_of((r * 2 + t) * band, 16)

    own = band_of(rep, tp)
    znb = band_of(rep, flip_tp)
    xnb = band_of(flip_rep, tp)
    dia = band_of(flip_rep, flip_tp)

    def both(c, b):
        return wbuf.at[c, :, pl.ds(b, band), :]

    Y, Z, X, DG, SB = range(5)

    def send(src, dst, ssem, rsem_, t, s, r):
        pltpu.make_async_remote_copy(
            src_ref=src, dst_ref=dst, send_sem=ssem, recv_sem=rsem_,
            device_id={"tp": t, "side": s, "rep": r}, device_id_type=MESH,
        ).start()

    def wait(ref, sem):
        pltpu.make_async_copy(ref, ref, sem).wait()

    def n_mod(l, m):
        return sum(1 for c in range(l * chunks, (l + 1) * chunks) if c % 3 == m)

    def piece_rows(t, rb, j):
        return pl.ds(pl.multiple_of(t * my_rows + rb * BLOCK + j * PIECE, PIECE), PIECE)

    @pl.when(side == 0)
    def _():
        rate = rate_ref[0]

        def loads(c):
            l, j = c // chunks, c % chunks
            cols = pl.ds(pl.multiple_of(j * UNIT, UNIT), UNIT)
            slot = c % LOAD_SLOTS
            return [
                pltpu.make_async_copy(r.at[l, :, cols], fin.at[slot, i], lsem.at[slot, i])
                for i, r in enumerate((w_up, g_up, w_dn, g_dn))
            ]

        for c in range(LOAD_SLOTS - 1):
            for cp in loads(c):
                cp.start()

        def send_chunk(c):
            slot = c % STAGE_SLOTS
            send(stage.at[slot], both(c, own), tss.at[slot, 0], rs.at[Y, c], tp, 1, rep)

            @pl.when(c % 3 == 0)
            def _():
                send(stage.at[slot], both(c, own), tss.at[slot, 1], rs.at[DG, c], flip_tp, 0, flip_rep)

        def wait_sent(c):
            slot = c % STAGE_SLOTS
            wait(stage.at[slot], tss.at[slot, 0])

            @pl.when(c % 3 == 0)
            def _():
                wait(stage.at[slot], tss.at[slot, 1])

        lag = 2

        def body(c, _):
            @pl.when(c < total)
            def _():
                @pl.when(c + LOAD_SLOTS - 1 < total)
                def _():
                    for cp in loads(c + LOAD_SLOTS - 1):
                        cp.start()

                for cp in loads(c):
                    cp.wait()
                slot, lslot = c % STAGE_SLOTS, c % LOAD_SLOTS

                @pl.when(c >= STAGE_SLOTS)
                def _():
                    wait_sent(c - STAGE_SLOTS)

                stage[slot, 0] = (fin[lslot, 0] - rate * fin[lslot, 1]).astype(jnp.bfloat16)
                stage[slot, 1] = (fin[lslot, 2] - rate * fin[lslot, 3]).astype(jnp.bfloat16)

            @pl.when((c >= 1) & (c < total + 1))
            def _():
                send_chunk(c - 1)

            @pl.when((c >= lag) & ((c - lag) % 3 == 0))
            def _():
                r = c - lag
                wait(both(r, dia), rs.at[DG, r])
                send(both(r, dia), both(r, dia), ss.at[0, r // chunks], rs.at[DG, r], tp, 1, rep)

            return 0

        lax.fori_loop(0, total + lag, body, 0)

        def drain(c, _):
            wait_sent(total - STAGE_SLOTS + c)
            return 0

        lax.fori_loop(0, STAGE_SLOTS, drain, 0)
        for l in range(layers):
            wait(wbuf.at[pl.ds(l * chunks, n_mod(l, 0)), :, pl.ds(0, band), :], ss.at[0, l])

        per = pieces // 2

        def relay(i, _):
            @pl.when(i < n_relay)
            def _():
                wait(rin.at[i], rsem.at[0, i])
                send(rin.at[i], rx.at[i], tss.at[0, 0], rsem.at[1, i], flip_tp, 0, rep)

            @pl.when(i >= 1)
            def _():
                q = i - 1
                wait(rx.at[q], rsem.at[1, q])
                rb, j = q // per, q % per
                send(rx.at[q], out.at[piece_rows(flip_tp, rb, j)], tss.at[1, 0],
                     osem.at[rb * pieces + j], tp, 1, rep)

            return 0

        lax.fori_loop(0, n_relay + 1, relay, 0)
        wait(rin.at[pl.ds(0, n_relay)], tss.at[0, 0])
        wait(rx.at[pl.ds(0, n_relay)], tss.at[1, 0])

    @pl.when(side == 1)
    def _():
        def y_stage(c):
            l = c // chunks
            wait(both(c, own), rs.at[Y, c])
            send(both(c, own), both(c, own), ss.at[0, l], rs.at[Z, c], flip_tp, 1, rep)
            send(both(c, own), both(c, own), ss.at[1, l], rs.at[X, c], tp, 1, flip_rep)
            send(both(c, own), both(c, own), ss.at[2, l], rs.at[SB, c], tp, 1, sib_rep)

        def n_stage(c):
            l = c // chunks
            wait(both(c, znb), rs.at[Z, c])

            @pl.when(c % 3 == 1)
            def _():
                send(both(c, znb), both(c, znb), ss.at[6, l], rs.at[DG, c], tp, 1, flip_rep)

            send(both(c, znb), both(c, znb), ss.at[3, l], rs.at[SB, c], tp, 1, sib_rep)
            wait(both(c, xnb), rs.at[X, c])

            @pl.when(c % 3 == 2)
            def _():
                send(both(c, xnb), both(c, xnb), ss.at[7, l], rs.at[DG, c], flip_tp, 1, rep)

            send(both(c, xnb), both(c, xnb), ss.at[4, l], rs.at[SB, c], tp, 1, sib_rep)

        def d_stage(c):
            wait(both(c, dia), rs.at[DG, c])
            send(both(c, dia), both(c, dia), ss.at[5, c // chunks], rs.at[SB, c], tp, 1, sib_rep)

        def s_wait(c):
            wait(wbuf.at[c, :, pl.ds(0, 4 * band), :], rs.at[SB, c])

        def wload(c, slot, j):
            return [
                pltpu.make_async_copy(
                    wbuf.at[c, m], wv.at[slot, m, :, pl.ds(j * UNIT, UNIT)], fsem.at[slot, j, m]
                )
                for m in range(2)
            ]

        def start(cps):
            for cp in cps:
                cp.start()

        def finish(cps):
            for cp in cps:
                cp.wait()

        def y_front(q):
            return jnp.minimum(total, 7 + q + q // 8)

        def n_front(q):
            return jnp.minimum(total, 5 + q + q // 9)

        def d_front(q):
            return jnp.minimum(total, 4 + q + q // 10)

        def run(fn, lo, hi):
            def body(c, _):
                fn(c)
                return 0

            lax.fori_loop(lo, hi, body, 0)

        def advance(q):
            run(y_stage, y_front(q), y_front(q + 1))
            run(n_stage, n_front(q), n_front(q + 1))
            run(d_stage, d_front(q), d_front(q + 1))

        def pload(b):
            rows = pl.ds(pl.multiple_of(tp * my_rows + b * BLOCK, BLOCK), BLOCK)
            return pltpu.make_async_copy(prompts.at[rows], rows_buf.at[b % 2], iosem.at[b % 2])

        pload(0).start()
        for b in range(blocks):
            if b + 1 < blocks:
                pload(b + 1).start()
            pload(b).wait()
            for j in range(pieces):
                h[b, :, pl.ds(j * PIECE, PIECE)] = rows_buf[b % 2, pl.ds(j * PIECE, PIECE), :].T

        for c in range(7):
            y_stage(c)
            if c >= 2:
                n_stage(c - 2)
            if c >= 3:
                d_stage(c - 3)
            if c >= 7 - lead:
                s_wait(c - (7 - lead))
                start(wload(c - (7 - lead), 0, c - (7 - lead)))

        def matmuls(slot, rb, width):
            a = lax.dot_general(
                wv[slot, 0, :, :width], h[rb], (((0,), (0,)), ((), ())), preferred_element_type=jnp.float32
            )
            u = gelu(a).astype(jnp.bfloat16)
            return jnp.dot(wv[slot, 1, :, :width], u, preferred_element_type=jnp.float32)

        def first_part(slot, rb):
            p[rb] = matmuls(slot, rb, lead * UNIT)

        def mid_part(slot, rb):
            p[rb] = p[rb] + matmuls(slot, rb, GROUP * UNIT)

        def last_part(slot, rb):
            s = p[rb] + matmuls(slot, rb, GROUP * UNIT)
            h[rb] = (h[rb].astype(jnp.float32) + s).astype(jnp.bfloat16)

        def group_step(l, g, width, n_next, part):
            step = l * groups + g
            slot = step % 2
            c0 = l * chunks + (0 if width == lead else lead + (g - 1) * GROUP)
            for j in range(width):
                finish(wload(c0 + j, slot, j))

            def block(rb, _):
                advance(step * blocks + rb)

                @pl.when(rb < n_next)
                def _():
                    c = c0 + width + rb
                    s_wait(c)
                    cols = pl.ds(pl.multiple_of(rb * UNIT, UNIT), UNIT)
                    for m in range(2):
                        pltpu.make_async_copy(
                            wbuf.at[c, m], wv.at[1 - slot, m, :, cols], fsem.at[1 - slot, rb, m]
                        ).start()

                part(slot, rb)
                return 0

            lax.fori_loop(0, blocks, block, 0)

        def layer_body(l, _):
            group_step(l, 0, lead, GROUP, first_part)

            def mid(g, _):
                group_step(l, g, GROUP, GROUP, mid_part)
                return 0

            lax.fori_loop(1, groups - 1, mid, 0)
            group_step(l, groups - 1, GROUP, lead, last_part)
            return 0

        lax.fori_loop(0, layers - 1, layer_body, 0)
        fine = (layers - 1) * groups * blocks
        run(y_stage, y_front(fine), total)
        run(n_stage, n_front(fine), total)
        run(d_stage, d_front(fine), total)
        run(s_wait, total - chunks + lead, total)

        c_last = total - chunks

        def group_chunk(g):
            return c_last + lead + (g - 1) * GROUP

        def load_group(c0, width, slot):
            for j in range(width):
                start(wload(c0 + j, slot, j))

        def wait_group(c0, width, slot):
            for j in range(width):
                finish(wload(c0 + j, slot, j))

        def put(rb, j):
            src = rows_buf.at[rb % 2, pl.ds(j * PIECE, PIECE), :]
            rows = piece_rows(tp, rb, j)
            pltpu.make_async_copy(src, out.at[rows], psem.at[rb % 2, j, 0]).start()
            by_relay = j < relays_of(rb, blocks, pieces)

            @pl.when(by_relay)
            def _():
                i = rb * (pieces // 2) + min(j, pieces // 2 - 1)
                send(src, rin.at[i], psem.at[rb % 2, j, 1], rsem.at[0, i], tp, 0, rep)

            @pl.when(jnp.logical_not(by_relay))
            def _():
                send(src, out.at[rows], psem.at[rb % 2, j, 1], osem.at[rb * pieces + j], flip_tp, 1, rep)

        def put_wait(rb):
            for j in range(pieces):
                src = rows_buf.at[rb % 2, pl.ds(j * PIECE, PIECE), :]
                wait(src, psem.at[rb % 2, j, 0])
                wait(src, psem.at[rb % 2, j, 1])

        def row_block(rb, _):
            step = (layers - 1) * groups + rb * groups
            slot = step % 2
            wait_group(c_last, lead, slot)
            load_group(c_last + lead, GROUP, 1 - slot)
            first_part(slot, rb)

            def mid(g, _):
                s = (step + g) % 2
                wait_group(group_chunk(g), GROUP, s)
                load_group(group_chunk(g + 1), GROUP, 1 - s)
                mid_part(s, rb)
                return 0

            lax.fori_loop(1, groups - 1, mid, 0)
            s = (step + groups - 1) % 2
            wait_group(group_chunk(groups - 1), GROUP, s)

            @pl.when(rb < blocks - 1)
            def _():
                load_group(c_last, lead, 1 - s)

            last_part(s, rb)

            @pl.when(rb >= 2)
            def _():
                put_wait(rb - 2)

            for j in range(pieces):
                cols = pl.ds(j * PIECE, PIECE)
                rows_buf[rb % 2, cols, :] = h[rb, :, cols].T
                if j >= 1:
                    put(rb, j - 1)
            put(rb, pieces - 1)
            return 0

        lax.fori_loop(0, blocks, row_block, 0)
        for rb in range(max(blocks - 2, 0), blocks):
            put_wait(rb)
        for i in range(blocks * pieces):
            wait(out.at[piece_rows(flip_tp, i // pieces, i % pieces)], osem.at[i])
        for l in range(layers):
            for i in range(8):
                n = n_mod(l, i - 5) if i >= 6 else chunks
                wait(wbuf.at[pl.ds(l * chunks, n), :, pl.ds(0, band), :], ss.at[i, l])


def finish_kernel(rate_ref, w_up, w_dn, g_up, g_dn, mid, new_up, new_dn, out, wb, gb, nb, ob, lsem, ssem, csem, zsem):
    layers, band, hidden = w_up.shape
    n_rows, d = out.shape
    slots, piece = ob.shape[:2]
    n_pieces = n_rows // piece
    side = lax.axis_index("side")
    arrays = ((w_up, g_up, new_up), (w_dn, g_dn, new_dn))
    work = [(a, l) for l in range(layers) for a in range(2)]

    @pl.when(side == 0)
    def _():
        rate = rate_ref[0]

        def load(i):
            a, l = work[i]
            return [
                pltpu.make_async_copy(arrays[a][0].at[l], wb.at[i % 2], lsem.at[i % 2, 0]),
                pltpu.make_async_copy(arrays[a][1].at[l], gb.at[i % 2], lsem.at[i % 2, 1]),
            ]

        def store(i):
            a, l = work[i]
            return pltpu.make_async_copy(nb.at[i % 2], arrays[a][2].at[l], ssem.at[i % 2])

        ob[0] = jnp.zeros(ob.shape[1:], ob.dtype)
        for cp in load(0):
            cp.start()
        for i in range(len(work)):
            if i + 1 < len(work):
                for cp in load(i + 1):
                    cp.start()
            for cp in load(i):
                cp.wait()
            if i >= 2:
                store(i - 2).wait()
            nb[i % 2] = wb[i % 2] - rate * gb[i % 2]
            store(i).start()
        zeros = [
            pltpu.make_async_copy(ob.at[0], out.at[pl.ds(i * piece, piece)], zsem.at[i]) for i in range(n_pieces)
        ]
        for cp in zeros:
            cp.start()
        for i in (len(work) - 2, len(work) - 1):
            store(i).wait()
        for cp in zeros:
            cp.wait()

    @pl.when(side == 1)
    def _():
        def load(i):
            return pltpu.make_async_copy(mid.at[pl.ds(i * piece, piece)], ob.at[i % slots], csem.at[i % slots, 0])

        def store(i):
            return pltpu.make_async_copy(ob.at[i % slots], out.at[pl.ds(i * piece, piece)], csem.at[i % slots, 1])

        for i in range(min(slots, n_pieces)):
            load(i).start()
        nb[0] = jnp.zeros(nb.shape[1:], nb.dtype)
        half = slots // 2
        for i in range(n_pieces):
            load(i).wait()
            store(i).start()
            n = i + half
            if i >= half and n < n_pieces:
                store(n - slots).wait()
                load(n).start()
        zeros = [
            pltpu.make_async_copy(nb.at[0], arrays[a][2].at[l], zsem.at[i]) for i, (a, l) in enumerate(work)
        ]
        for cp in zeros:
            cp.start()
        for i in range(max(n_pieces - slots, 0), n_pieces):
            store(i).wait()
        for cp in zeros:
            cp.wait()


def solution(mesh):
    up_spec = P("side", None, ("rep", "tp"), None)
    down_spec = P("side", None, None, ("rep", "tp"))
    tok_spec = P("side", "rep", None, None)

    def device_step(w_up, w_down, g_up, g_down, learn_rate, prompts):
        layers, band, hidden = w_up.shape[1:]
        n_rows, d = prompts.shape[2:]
        chunks = hidden // UNIT
        total = layers * chunks
        my_rows = n_rows // 2
        blocks, pieces = my_rows // BLOCK, BLOCK // PIECE
        weights = (w_up[0], jnp.swapaxes(w_down[0], 1, 2), g_up[0], jnp.swapaxes(g_down[0], 1, 2))
        smem = pl.BlockSpec(memory_space=pltpu.SMEM)
        hbm = pl.BlockSpec(memory_space=pl.ANY)
        bf16 = jnp.bfloat16
        relay = jax.ShapeDtypeStruct((blocks * pieces // 2, PIECE, d), bf16)
        rows_out, _, _, _ = pl.pallas_call(
            sync_kernel,
            name="sync_and_forward",
            out_shape=(
                jax.ShapeDtypeStruct((n_rows, d), bf16),
                jax.ShapeDtypeStruct((total, 2, d, UNIT), bf16),
                relay,
                relay,
            ),
            in_specs=[smem] + [hbm] * 5,
            out_specs=(hbm,) * 4,
            scratch_shapes=[
                pltpu.VMEM((blocks, d, BLOCK), bf16),
                pltpu.VMEM((blocks, d, BLOCK), jnp.float32),
                pltpu.VMEM((2, 2, d, GROUP * UNIT), bf16),
                pltpu.VMEM((LOAD_SLOTS, 4, band, UNIT), jnp.float32),
                pltpu.VMEM((STAGE_SLOTS, 2, band, UNIT), bf16),
                pltpu.VMEM((2, BLOCK, d), bf16),
                pltpu.SemaphoreType.DMA((5, total)),
                pltpu.SemaphoreType.DMA((8, layers)),
                pltpu.SemaphoreType.DMA((LOAD_SLOTS, 4)),
                pltpu.SemaphoreType.DMA((2, GROUP, 2)),
                pltpu.SemaphoreType.DMA((STAGE_SLOTS, 2)),
                pltpu.SemaphoreType.DMA((2,)),
                pltpu.SemaphoreType.DMA((2, pieces, 2)),
                pltpu.SemaphoreType.DMA((blocks * pieces,)),
                pltpu.SemaphoreType.DMA((2, blocks * pieces // 2)),
            ],
            compiler_params=pltpu.CompilerParams(has_side_effects=True, vmem_limit_bytes=60 * 1024 * 1024),
        )(learn_rate, *weights, prompts[0, 0])
        piece = n_rows // 16
        new_up, new_dn, gen_out = pl.pallas_call(
            finish_kernel,
            name="write_outputs",
            out_shape=(
                jax.ShapeDtypeStruct((layers, band, hidden), jnp.float32),
                jax.ShapeDtypeStruct((layers, band, hidden), jnp.float32),
                jax.ShapeDtypeStruct((n_rows, d), bf16),
            ),
            in_specs=[smem] + [hbm] * 5,
            out_specs=(hbm,) * 3,
            scratch_shapes=[
                pltpu.VMEM((2, band, hidden), jnp.float32),
                pltpu.VMEM((2, band, hidden), jnp.float32),
                pltpu.VMEM((2, band, hidden), jnp.float32),
                pltpu.VMEM((8, piece, d), bf16),
                pltpu.SemaphoreType.DMA((2, 2)),
                pltpu.SemaphoreType.DMA((2,)),
                pltpu.SemaphoreType.DMA((8, 2)),
                pltpu.SemaphoreType.DMA((max(16, 2 * layers),)),
            ],
            compiler_params=pltpu.CompilerParams(vmem_limit_bytes=62 * 1024 * 1024),
        )(learn_rate, *weights, rows_out)
        return new_up[None], jnp.swapaxes(new_dn, 1, 2)[None], gen_out[None, None]

    return jax.shard_map(
        device_step,
        mesh=mesh,
        in_specs=(up_spec, down_spec, up_spec, down_spec, P("side"), tok_spec),
        out_specs=(up_spec, down_spec, tok_spec),
        check_vma=False,
    )
```

time: 5420 us -> 663 us (0.12)
  waiting for transfers between devices: 4240 us -> 0 us
  matrix products: 726 us -> 0 us
  Pallas kernels: 0 us -> 662 us
  blocking collectives: 240 us -> 0 us
  other arithmetic: 116 us -> 0 us
  local copies, waits for them, and re-layouts: 71.8 us -> 0 us
    psum x6 -> x0, waiting for transfers between devices: 3860 us -> none  [device_step(): part_sum = lax.psum(part_sum, 'tp')]
    dot_general x12 -> x0, matrix products: 726 us -> none  [the longest x6 412 us: device_step(): jnp.dot(hidden, full_up[layer], preferred_element_type=jnp.float32)]
    pallas_call x0 -> x2, Pallas kernels: none -> 662 us  [the longest x1 631 us: device_step(): pl.pallas_call(sync_kernel, name='sync_and_forward', out_shape=(jax.Shape...]
    ppermute x2 -> x0, waiting for transfers between devices: 273 us -> none  [the longest x1 137 us: device_step(): lax.ppermute(new_up[0].astype(jnp.bfloat16), 'side', perm=[(0, 1)])]
    all_to_all x2 -> x0, blocking collectives: 240 us -> none  [the longest x1 121 us: device_step(): band_up = lax.all_to_all(recv_up, 'tp', 2, 1, tiled=True)]
    all_gather x2 -> x0, waiting for transfers between devices: 99 us -> none  [the longest x1 99 us: device_step(): full_down = lax.all_gather(band_down, 'rep', axis=2, tiled=True)]
    convert_element_type x4 -> x0, other arithmetic: 86.6 us -> none  [the longest x2 57.7 us: device_step(): hidden = (hidden.astype(jnp.float32) + part_sum).astype(jnp.bfloat16)]
  transfers between devices with their start and end apart: 10 -> 0, of which waited for: 9 -> 0; matrix products, arithmetic and copies ran while one was open for 2% -> 0% of each run, Pallas kernels for 0% -> 0%
where the time goes in v3:
time: 663 us
  Pallas kernels  662 us (100%)
    pallas_call x1, Pallas kernels, device_step(): pl.pallas_call(sync_kernel, name='sync_and_forward', out_shape=(jax.Shape...  631 us
    pallas_call x1, Pallas kernels, device_step(): pl.pallas_call(finish_kernel, name='write_outputs', out_shape=(jax.ShapeD...  30.8 us

profile of v3, /device:TPU:0, one launch (start us, length us, event | category | flops | bytes accessed | tf_op | source)
XLA Modules:
  0.0 663.1 jit_solution(15028899765045916668)
XLA Ops:
  1.3 630.8 %sync_and_forward.1 = (bf16[8192,896]{1,0:T(8,128)(2,1)}, bf16[114,2,896,256]{3,2,1,0:T(8,128)(2,1)}, bf16[16,128,896]{2,1,0:T(8,128)(2,1)}, bf16[16,128,896]{2,1,0:T(8,128)(2,1)}) custom-call(f32[1]{0:T(128)S(6)} %copy.9.rate_ref, f32[6,112,4864]{2,1,0:T(8,128)} %bitcast.14, f32[6,112,4864]{2,1,0:T(8,128)} %bitcast.16, f32[6,112,4864]{2,1,0:T(8,128)} %bitcast.18, ...), custom_call_target="tpu_custom_call" | custom-call | tf_op jit(solution)/shard_map/sync_and_forward/pallas_call | solution.py:504
  632.1 30.8 %write_outputs.1 = (f32[6,112,4864]{2,1,0:T(8,128)}, f32[6,112,4864]{2,1,0:T(8,128)}, bf16[8192,896]{1,0:T(8,128)(2,1)}) custom-call(f32[1]{0:T(128)S(6)} %copy.9.rate_ref, f32[6,112,4864]{2,1,0:T(8,128)} %bitcast.15, f32[6,112,4864]{2,1,0:T(8,128)} %bitcast.17, f32[6,112,4864]{2,1,0:T(8,128)} %bitcast.19, f32[6,112,4864]{2,1,0:T(8,128)} %bitcast.21, ...), custom_call_target="tpu_custom_call" | custom-call | tf_op jit(solution)/shard_map/write_outputs/pallas_call | solution.py:535

commit v4 on v3

v4 whole, which is shorter than its diff:
```python
import jax
import jax.numpy as jnp
from jax import lax
from jax.experimental import pallas as pl
from jax.experimental.pallas import tpu as pltpu
from jax.sharding import PartitionSpec as P

MESH = pl.DeviceIdType.MESH
UNIT = 256
GROUP = 4
BLOCK = 1024
PIECE = 128
LOAD_SLOTS = 4
STAGE_SLOTS = 12
AHEAD = 3
GELU_A = 0.7978845608028654
GELU_B = 0.7978845608028654 * 0.044715


def gelu(a):
    return a * (0.5 * jnp.tanh(a * (GELU_A + GELU_B * (a * a))) + 0.5)


def relays_of(rb, blocks, pieces):
    return pieces // 2 - (rb == blocks - 1).astype(jnp.int32)


def sync_kernel(
    rate_ref, w_up, w_dn, g_up, g_dn, prompts, out, nu, nd, wbuf, rin, rx,
    h, p, wv, fin, fnew, stage, rows_buf,
    rs, ss, lsem, fsem, tss, iosem, psem, osem, rsem,
):
    layers, band, hidden = w_up.shape
    chunks = hidden // UNIT
    total = layers * chunks
    groups = -(-chunks // GROUP)
    lead = chunks - (groups - 1) * GROUP
    n_rows, d = out.shape
    my_rows = n_rows // 2
    blocks = my_rows // BLOCK
    pieces = BLOCK // PIECE
    n_relay = blocks * (pieces // 2) - 1

    tp = lax.axis_index("tp")
    side = lax.axis_index("side")
    rep = lax.axis_index("rep")
    x, k = rep // 2, rep % 2
    flip_tp = 1 - tp
    flip_rep = (1 - x) * 2 + k
    sib_rep = x * 2 + (1 - k)

    own, znb, xnb, dia = (x, tp), (x, flip_tp), (1 - x, tp), (1 - x, flip_tp)

    def both(c, b):
        return wbuf.at[c, :, b[0], k, b[1]]

    Y, Z, X, DG, SB = range(5)

    def send(src, dst, ssem, rsem_, t, s, r):
        pltpu.make_async_remote_copy(
            src_ref=src, dst_ref=dst, send_sem=ssem, recv_sem=rsem_,
            device_id={"tp": t, "side": s, "rep": r}, device_id_type=MESH,
        ).start()

    def wait(ref, sem):
        pltpu.make_async_copy(ref, ref, sem).wait()

    def start(cps):
        for cp in cps:
            cp.start()

    def finish(cps):
        for cp in cps:
            cp.wait()

    def n_mod(l, m):
        return sum(1 for c in range(l * chunks, (l + 1) * chunks) if c % 3 == m)

    def piece_rows(t, rb, j):
        return pl.ds(pl.multiple_of(t * my_rows + rb * BLOCK + j * PIECE, PIECE), PIECE)

    @pl.when(side == 0)
    def _():
        rate = rate_ref[0]
        parts = ((w_up, g_up, nu), (w_dn, g_dn, nd))

        def cols_of(c):
            return c // chunks, pl.ds(pl.multiple_of((c % chunks) * UNIT, UNIT), UNIT)

        def loads(c):
            l, cols = cols_of(c)
            slot = c % LOAD_SLOTS
            return [
                pltpu.make_async_copy(r.at[l, :, cols], fin.at[slot, 2 * m + i], lsem.at[slot, 2 * m + i])
                for m in range(2)
                for i, r in enumerate(parts[m][:2])
            ]

        def stores(c):
            l, cols = cols_of(c)
            slot = c % LOAD_SLOTS
            return [
                pltpu.make_async_copy(fnew.at[slot, m], parts[m][2].at[l, :, cols], fsem.at[slot // 2, slot % 2, m])
                for m in range(2)
            ]

        for c in range(LOAD_SLOTS - 1):
            start(loads(c))

        def send_own(c):
            send(stage.at[c % STAGE_SLOTS], both(c, own), tss.at[c % STAGE_SLOTS, 0], rs.at[Y, c], tp, 1, rep)

        def send_dia(c):
            send(stage.at[c % STAGE_SLOTS], both(c, own), tss.at[c % STAGE_SLOTS, 1], rs.at[DG, c], flip_tp, 0, flip_rep)

        def wait_sent(c):
            slot = c % STAGE_SLOTS
            wait(stage.at[slot], tss.at[slot, 0])

            @pl.when(c % 3 == 0)
            def _():
                wait(stage.at[slot], tss.at[slot, 1])

        def body(c, _):
            @pl.when(c < total)
            def _():
                @pl.when(c + LOAD_SLOTS - 1 < total)
                def _():
                    start(loads(c + LOAD_SLOTS - 1))

                finish(loads(c))
                slot, lslot = c % STAGE_SLOTS, c % LOAD_SLOTS

                @pl.when(c >= STAGE_SLOTS)
                def _():
                    wait_sent(c - STAGE_SLOTS)

                @pl.when(c >= LOAD_SLOTS)
                def _():
                    finish(stores(c - LOAD_SLOTS))

                for m in range(2):
                    new = fin[lslot, 2 * m] - rate * fin[lslot, 2 * m + 1]
                    fnew[lslot, m] = new
                    stage[slot, m] = new.astype(jnp.bfloat16)

            @pl.when((c >= 1) & (c < total + 1))
            def _():
                start(stores(c - 1))

                @pl.when((c - 1) % 3 == 0)
                def _():
                    send_dia(c - 1)

            r = c - 1 - AHEAD

            @pl.when(r >= 0)
            def _():
                send_own(r)

                @pl.when(r % 3 == 0)
                def _():
                    wait(both(r, dia), rs.at[DG, r])
                    send(both(r, dia), both(r, dia), ss.at[0, r // chunks], rs.at[DG, r], tp, 1, rep)

            return 0

        lax.fori_loop(0, total + 1 + AHEAD, body, 0)

        def drain(c, _):
            wait_sent(total - STAGE_SLOTS + c)
            return 0

        lax.fori_loop(0, STAGE_SLOTS, drain, 0)
        for c in range(total - LOAD_SLOTS, total):
            finish(stores(c))
        for l in range(layers):
            wait(wbuf.at[pl.ds(l * chunks, n_mod(l, 0)), :, 0, 0, 0], ss.at[0, l])

        per = pieces // 2

        def relay(i, _):
            @pl.when(i < n_relay)
            def _():
                wait(rin.at[i], rsem.at[0, i])
                send(rin.at[i], rx.at[i], tss.at[0, 0], rsem.at[1, i], flip_tp, 0, rep)

            @pl.when(i >= 1)
            def _():
                q = i - 1
                wait(rx.at[q], rsem.at[1, q])
                rb, j = q // per, q % per
                send(rx.at[q], out.at[piece_rows(flip_tp, rb, j)], tss.at[1, 0],
                     osem.at[rb * pieces + j], tp, 1, rep)

            return 0

        lax.fori_loop(0, n_relay + 1, relay, 0)
        wait(rin.at[pl.ds(0, n_relay)], tss.at[0, 0])
        wait(rx.at[pl.ds(0, n_relay)], tss.at[1, 0])

    @pl.when(side == 1)
    def _():
        def y_stage(c):
            l = c // chunks
            wait(both(c, own), rs.at[Y, c])
            send(both(c, own), both(c, own), ss.at[0, l], rs.at[Z, c], flip_tp, 1, rep)
            send(both(c, own), both(c, own), ss.at[1, l], rs.at[X, c], tp, 1, flip_rep)

        def n_stage(c):
            l = c // chunks
            wait(both(c, znb), rs.at[Z, c])

            @pl.when(c % 3 == 1)
            def _():
                send(both(c, znb), both(c, znb), ss.at[2, l], rs.at[DG, c], tp, 1, flip_rep)

            wait(both(c, xnb), rs.at[X, c])

            @pl.when(c % 3 == 2)
            def _():
                send(both(c, xnb), both(c, xnb), ss.at[3, l], rs.at[DG, c], flip_tp, 1, rep)

        def core_half(c, core):
            return wbuf.at[c, :, :, core]

        def d_stage(c):
            wait(both(c, dia), rs.at[DG, c])
            send(core_half(c, k), core_half(c, k), ss.at[4, c // chunks], rs.at[SB, c], tp, 1, sib_rep)

        def s_wait(c):
            wait(core_half(c, 1 - k), rs.at[SB, c])

        def wload(c, slot, j):
            cols = pl.ds(j * UNIT if isinstance(j, int) else pl.multiple_of(j * UNIT, UNIT), UNIT)
            return [
                pltpu.make_async_copy(wbuf.at[c, m], wv.at[slot, m, :, :, :, :, cols], fsem.at[slot, j, m])
                for m in range(2)
            ]

        def y_front(q):
            return jnp.minimum(total, 8 + q + q // 5)

        def n_front(q):
            return jnp.minimum(total, 6 + q + q // 6)

        def d_front(q):
            return jnp.minimum(total, 4 + q + q // 10)

        def run(fn, lo, hi):
            def body(c, _):
                fn(c)
                return 0

            lax.fori_loop(lo, hi, body, 0)

        def pload(b):
            rows = pl.ds(pl.multiple_of(tp * my_rows + b * BLOCK, BLOCK), BLOCK)
            return pltpu.make_async_copy(prompts.at[rows], rows_buf.at[b % 2], iosem.at[b % 2])

        pload(0).start()
        for b in range(blocks):
            if b + 1 < blocks:
                pload(b + 1).start()
            pload(b).wait()
            for j in range(pieces):
                h[b, :, pl.ds(j * PIECE, PIECE)] = rows_buf[b % 2, pl.ds(j * PIECE, PIECE), :].T

        for c in range(8):
            y_stage(c)
            if c >= 2:
                n_stage(c - 2)
            if c >= 4:
                d_stage(c - 4)
            if c >= 8 - lead:
                s_wait(c - (8 - lead))
                start(wload(c - (8 - lead), 0, c - (8 - lead)))

        def matmuls(slot, rb, width):
            def weight(m):
                return wv[slot, m, :, :, :, :, : width * UNIT].reshape(d, width * UNIT)

            a = lax.dot_general(weight(0), h[rb], (((0,), (0,)), ((), ())), preferred_element_type=jnp.float32)
            u = gelu(a).astype(jnp.bfloat16)
            return jnp.dot(weight(1), u, preferred_element_type=jnp.float32)

        def put(rb, j):
            src = rows_buf.at[rb % 2, pl.ds(j * PIECE, PIECE), :]
            rows = piece_rows(tp, rb, j)
            pltpu.make_async_copy(src, out.at[rows], psem.at[rb % 2, j, 0]).start()
            by_relay = j < relays_of(rb, blocks, pieces)

            @pl.when(by_relay)
            def _():
                i = rb * (pieces // 2) + min(j, pieces // 2 - 1)
                send(src, rin.at[i], psem.at[rb % 2, j, 1], rsem.at[0, i], tp, 0, rep)

            @pl.when(jnp.logical_not(by_relay))
            def _():
                send(src, out.at[rows], psem.at[rb % 2, j, 1], osem.at[rb * pieces + j], flip_tp, 1, rep)

        def put_wait(rb):
            for j in range(pieces):
                src = rows_buf.at[rb % 2, pl.ds(j * PIECE, PIECE), :]
                wait(src, psem.at[rb % 2, j, 0])
                wait(src, psem.at[rb % 2, j, 1])

        per_layer = groups * blocks
        turn = (layers - 1) * per_layer

        def visit(t, _):
            early = t < turn
            late = t - turn
            l = jnp.where(early, t // per_layer, layers - 1)
            g = jnp.where(early, (t % per_layer) // blocks, late % groups)
            rb = jnp.where(early, t % blocks, late // groups)
            use = jnp.where(early, t // blocks, (layers - 1) * groups + late)
            slot = use % 2
            width = jnp.where(g == 0, lead, GROUP)
            c0 = l * chunks + jnp.where(g == 0, 0, lead + (g - 1) * GROUP)

            @pl.when(jnp.logical_not(early) | (rb == 0))
            def _():
                for j in range(GROUP):

                    @pl.when(j < width)
                    def _():
                        finish(wload(c0 + j, slot, j))

            @pl.when(early)
            def _():
                run(y_stage, y_front(t), y_front(t + 1))
                run(n_stage, n_front(t), n_front(t + 1))
                run(d_stage, d_front(t), d_front(t + 1))

                @pl.when(rb < jnp.where(g == groups - 1, lead, GROUP))
                def _():
                    s_wait(c0 + width + rb)
                    start(wload(c0 + width + rb, 1 - slot, rb))

            @pl.when(t == turn)
            def _():
                run(y_stage, y_front(turn), total)
                run(n_stage, n_front(turn), total)
                run(d_stage, d_front(turn), total)
                run(s_wait, total - chunks + lead, total)

            @pl.when(jnp.logical_not(early) & (late < per_layer - 1))
            def _():
                wrap = g == groups - 1
                n0 = jnp.where(wrap, total - chunks, c0 + width)
                for j in range(GROUP):

                    @pl.when(j < jnp.where(wrap, lead, GROUP))
                    def _():
                        start(wload(n0 + j, 1 - slot, j))

            @pl.when(g == 0)
            def _():
                p[rb] = matmuls(slot, rb, lead)

            @pl.when((g > 0) & (g < groups - 1))
            def _():
                p[rb] = p[rb] + matmuls(slot, rb, GROUP)

            @pl.when(g == groups - 1)
            def _():
                s = p[rb] + matmuls(slot, rb, GROUP)
                h[rb] = (h[rb].astype(jnp.float32) + s).astype(jnp.bfloat16)

            @pl.when(jnp.logical_not(early) & (g == groups - 1))
            def _():
                @pl.when(rb >= 2)
                def _():
                    put_wait(rb - 2)

                for j in range(pieces):
                    cols = pl.ds(j * PIECE, PIECE)
                    rows_buf[rb % 2, cols, :] = h[rb, :, cols].T
                    if j >= 1:
                        put(rb, j - 1)
                put(rb, pieces - 1)

            return 0

        lax.fori_loop(0, layers * per_layer, visit, 0)
        for rb in range(max(blocks - 2, 0), blocks):
            put_wait(rb)
        for i in range(blocks * pieces):
            wait(out.at[piece_rows(flip_tp, i // pieces, i % pieces)], osem.at[i])
        for l in range(layers):
            for i in range(5):
                if i == 4:
                    wait(wbuf.at[pl.ds(l * chunks, chunks), :, :, 0], ss.at[i, l])
                else:
                    n = n_mod(l, i - 1) if i >= 2 else chunks
                    wait(wbuf.at[pl.ds(l * chunks, n), :, 0, 0, 0], ss.at[i, l])


def finish_kernel(up, dn, rows, new_up, new_dn, out, buf, zbuf, lsem, ssem, zsem):
    layers = up.shape[0]
    n_rows = rows.shape[0]
    slots, band, hidden = buf.shape
    side = lax.axis_index("side")
    items = [(i, o, l) for l in range(layers) for i, o in ((up, new_up), (dn, new_dn))]
    piece = zbuf.shape[1]
    n_pieces = n_rows // piece
    n_slots = zbuf.shape[0]

    def pipeline(n, n_slots, load, store):
        for i in range(min(n_slots, n)):
            load(i).start()
        half = n_slots // 2
        for i in range(n):
            load(i).wait()
            store(i).start()
            nxt = i + half
            if i >= half and nxt < n:
                store(nxt - n_slots).wait()
                load(nxt).start()

    @pl.when(side == 0)
    def _():
        zbuf[0] = jnp.zeros(zbuf.shape[1:], zbuf.dtype)
        zeros = [
            pltpu.make_async_copy(zbuf.at[0], out.at[pl.ds(i * piece, piece)], zsem.at[i]) for i in range(n_pieces)
        ]
        for cp in zeros:
            cp.start()

        def load(i):
            src, _, l = items[i]
            return pltpu.make_async_copy(src.at[l], buf.at[i % slots], lsem.at[i % slots])

        def store(i):
            _, dst, l = items[i]
            return pltpu.make_async_copy(buf.at[i % slots], dst.at[l], ssem.at[i % slots])

        n = len(items)
        pipeline(n, slots, load, store)
        for i in range(max(n - slots, 0), n):
            store(i).wait()
        for cp in zeros:
            cp.wait()

    @pl.when(side == 1)
    def _():
        buf[0] = jnp.zeros(buf.shape[1:], buf.dtype)
        zeros = [pltpu.make_async_copy(buf.at[0], dst.at[l], zsem.at[i]) for i, (_, dst, l) in enumerate(items)]
        for cp in zeros:
            cp.start()

        def load(i):
            return pltpu.make_async_copy(rows.at[pl.ds(i * piece, piece)], zbuf.at[i % n_slots], lsem.at[i % n_slots])

        def store(i):
            return pltpu.make_async_copy(zbuf.at[i % n_slots], out.at[pl.ds(i * piece, piece)], ssem.at[i % n_slots])

        pipeline(n_pieces, n_slots, load, store)
        for i in range(max(n_pieces - n_slots, 0), n_pieces):
            store(i).wait()
        for cp in zeros:
            cp.wait()


def solution(mesh):
    up_spec = P("side", None, ("rep", "tp"), None)
    down_spec = P("side", None, None, ("rep", "tp"))
    tok_spec = P("side", "rep", None, None)

    def device_step(w_up, w_down, g_up, g_down, learn_rate, prompts):
        layers, band, hidden = w_up.shape[1:]
        n_rows, d = prompts.shape[2:]
        chunks = hidden // UNIT
        total = layers * chunks
        my_rows = n_rows // 2
        blocks, pieces = my_rows // BLOCK, BLOCK // PIECE
        weights = (w_up[0], jnp.swapaxes(w_down[0], 1, 2), g_up[0], jnp.swapaxes(g_down[0], 1, 2))
        smem = pl.BlockSpec(memory_space=pltpu.SMEM)
        hbm = pl.BlockSpec(memory_space=pl.ANY)
        bf16 = jnp.bfloat16
        relay = jax.ShapeDtypeStruct((blocks * pieces // 2, PIECE, d), bf16)
        new_w = jax.ShapeDtypeStruct((layers, band, hidden), jnp.float32)
        rows = jax.ShapeDtypeStruct((n_rows, d), bf16)
        rows_mid, up_mid, dn_mid, _, _, _ = pl.pallas_call(
            sync_kernel,
            name="sync_and_forward",
            out_shape=(
                rows,
                new_w,
                new_w,
                jax.ShapeDtypeStruct((total, 2, 2, 2, 2, band, UNIT), bf16),
                relay,
                relay,
            ),
            in_specs=[smem] + [hbm] * 5,
            out_specs=(hbm,) * 6,
            scratch_shapes=[
                pltpu.VMEM((blocks, d, BLOCK), bf16),
                pltpu.VMEM((blocks, d, BLOCK), jnp.float32),
                pltpu.VMEM((2, 2, 2, 2, 2, band, GROUP * UNIT), bf16),
                pltpu.VMEM((LOAD_SLOTS, 4, band, UNIT), jnp.float32),
                pltpu.VMEM((LOAD_SLOTS, 2, band, UNIT), jnp.float32),
                pltpu.VMEM((STAGE_SLOTS, 2, band, UNIT), bf16),
                pltpu.VMEM((2, BLOCK, d), bf16),
                pltpu.SemaphoreType.DMA((5, total)),
                pltpu.SemaphoreType.DMA((5, layers)),
                pltpu.SemaphoreType.DMA((LOAD_SLOTS, 4)),
                pltpu.SemaphoreType.DMA((2, GROUP, 2)),
                pltpu.SemaphoreType.DMA((STAGE_SLOTS, 2)),
                pltpu.SemaphoreType.DMA((2,)),
                pltpu.SemaphoreType.DMA((2, pieces, 2)),
                pltpu.SemaphoreType.DMA((blocks * pieces,)),
                pltpu.SemaphoreType.DMA((2, blocks * pieces // 2)),
            ],
            compiler_params=pltpu.CompilerParams(has_side_effects=True, vmem_limit_bytes=60 * 1024 * 1024),
        )(learn_rate, *weights, prompts[0, 0])
        new_up, new_dn, gen_out = pl.pallas_call(
            finish_kernel,
            name="write_outputs",
            out_shape=(new_w, new_w, rows),
            in_specs=[hbm] * 3,
            out_specs=(hbm,) * 3,
            scratch_shapes=[
                pltpu.VMEM((8, band, hidden), jnp.float32),
                pltpu.VMEM((8, n_rows // 16, d), bf16),
                pltpu.SemaphoreType.DMA((8,)),
                pltpu.SemaphoreType.DMA((8,)),
                pltpu.SemaphoreType.DMA((max(16, 2 * layers),)),
            ],
            compiler_params=pltpu.CompilerParams(vmem_limit_bytes=62 * 1024 * 1024),
        )(up_mid, dn_mid, rows_mid)
        return new_up[None], jnp.swapaxes(new_dn, 1, 2)[None], gen_out[None, None]

    return jax.shard_map(
        device_step,
        mesh=mesh,
        in_specs=(up_spec, down_spec, up_spec, down_spec, P("side"), tok_spec),
        out_specs=(up_spec, down_spec, tok_spec),
        check_vma=False,
    )
```

time: 663 us -> 620 us (0.935)
  Pallas kernels: 662 us -> 618 us
    pallas_call x2, Pallas kernels: 662 us -> 618 us  [the longest x1 595 us: device_step(): pl.pallas_call(sync_kernel, name='sync_and_forward', out_shape=(rows, new...]
where the time goes in v4:
time: 620 us
  Pallas kernels  618 us (100%)
    pallas_call x1, Pallas kernels, device_step(): pl.pallas_call(sync_kernel, name='sync_and_forward', out_shape=(rows, new...  595 us
    pallas_call x1, Pallas kernels, device_step(): pl.pallas_call(finish_kernel, name='write_outputs', out_shape=(new_w, new...  23.2 us

profile of v4, /device:TPU:0, one launch (start us, length us, event | category | flops | bytes accessed | tf_op | source)
XLA Modules:
  0.0 619.9 jit_solution(16167625239724819048)
XLA Ops:
  1.3 595.2 %sync_and_forward.1 = (bf16[8192,896]{1,0:T(8,128)(2,1)}, f32[6,112,4864]{2,1,0:T(8,128)}, f32[6,112,4864]{2,1,0:T(8,128)}, bf16[114,2,2,2,2,112,256]{6,5,4,3,2,...) custom-call(f32[1]{0:T(128)S(6)} %copy.9.rate_ref, f32[6,112,4864]{2,1,0:T(8,128)} %bitcast.15, ...), custom_call_target="tpu_custom_call" | custom-call | tf_op jit(solution)/shard_map/sync_and_forward/pallas_call | solution.py:485
  596.5 23.2 %write_outputs.1 = (f32[6,112,4864]{2,1,0:T(8,128)}, f32[6,112,4864]{2,1,0:T(8,128)}, bf16[8192,896]{1,0:T(8,128)(2,1)}) custom-call(f32[6,112,4864]{2,1,0:T(8,128)} %get-tuple-element.9.up, f32[6,112,4864]{2,1,0:T(8,128)} %get-tuple-element.10.dn, bf16[8192,896]{1,0:T(8,128)(2,1)} %get-tuple-element.11.rows), custom_call_target="tpu_custom_call" | custom-call | tf_op jit(solution)/shard_map/write_outputs/pallas_call | solution.py:518

commit v5 on v4

v5 whole, which is shorter than its diff:
```python
import jax
import jax.numpy as jnp
from jax import lax
from jax.experimental import pallas as pl
from jax.experimental.pallas import tpu as pltpu
from jax.sharding import PartitionSpec as P

MESH = pl.DeviceIdType.MESH
UNIT = 256
GROUP = 5
BLOCK = 512
PIECE = 128
EARLY = 2
LOAD_SLOTS = 4
STAGE_SLOTS = 12
RELAY_LAG = 4
FIRST_LATE = 2
RELAY_BLOCK = 6
FRONTS = ((10, 15, 7, 44), (8, 14, 2, 48), (6, 13, 3, 56))
GELU_A = 0.7978845608028654
GELU_B = 0.7978845608028654 * 0.044715


def gelu(a):
    return a * (0.5 * jnp.tanh(a * (GELU_A + GELU_B * (a * a))) + 0.5)


def sync_kernel(
    rate_ref, w_up, w_dn, g_up, g_dn, prompts, out, nu, nd, wbuf, rin, rx,
    h, p, wv, fin, fnew, stage, rows_buf,
    rs, ss, lsem, fsem, tss, csem, iosem, psem, osem, rsem, hs, hr,
):
    layers, band, hidden = w_up.shape
    chunks = hidden // UNIT
    groups = -(-chunks // GROUP)
    lead = chunks - (groups - 1) * GROUP
    mid = EARLY * chunks
    gen = 2 * mid
    n_rows, d = out.shape
    my_rows = n_rows // 2
    blocks = my_rows // BLOCK
    pieces = BLOCK // PIECE

    tp = lax.axis_index("tp")
    side = lax.axis_index("side")
    rep = lax.axis_index("rep")
    x, k = rep // 2, rep % 2
    flip_tp = 1 - tp
    flip_rep = (1 - x) * 2 + k
    sib_rep = x * 2 + (1 - k)

    own, znb, xnb, dia = (x, tp), (x, flip_tp), (1 - x, tp), (1 - x, flip_tp)

    def both(c, b):
        return wbuf.at[c, :, b[0], k, b[1]]

    def core_half(c, core):
        return wbuf.at[c, :, :, core]

    def chunk_of(e):
        return e + jnp.where(e >= mid, mid, 0)

    def relayed(e):
        return e % 5 == 4

    Y, Z, X, DG, SB = range(5)

    def send(src, dst, ssem, rsem_, t, s, r):
        pltpu.make_async_remote_copy(
            src_ref=src, dst_ref=dst, send_sem=ssem, recv_sem=rsem_,
            device_id={"tp": t, "side": s, "rep": r}, device_id_type=MESH,
        ).start()

    def wait(ref, sem):
        pltpu.make_async_copy(ref, ref, sem).wait()

    def start(cps):
        for cp in cps:
            cp.start()

    def finish(cps):
        for cp in cps:
            cp.wait()

    def run(fn, lo, hi):
        def body(c, _):
            fn(c)
            return 0

        lax.fori_loop(lo, hi, body, 0)

    def piece_rows(t, b, j):
        return pl.ds(pl.multiple_of(t * my_rows + b * BLOCK + j * PIECE, PIECE), PIECE)

    def s_wait(c):
        wait(core_half(c, 1 - k), rs.at[SB, c])

    def wload(c, slot, j):
        cols = pl.ds(j * UNIT if isinstance(j, int) else pl.multiple_of(j * UNIT, UNIT), UNIT)
        return [
            pltpu.make_async_copy(wbuf.at[c, m], wv.at[slot, m, :, :, :, :, cols], fsem.at[slot, j, m])
            for m in range(2)
        ]

    def each_chunk(c0, width, fn):
        for j in range(GROUP):

            @pl.when(j < width)
            def _():
                fn(c0 + j, j)

    def width_of(g):
        return jnp.where(g == 0, lead, GROUP)

    def first_of(l, g):
        return l * chunks + jnp.where(g == 0, 0, lead + (g - 1) * GROUP)

    def matmuls(slot, hb, width):
        def weight(m):
            return wv[slot, m, :, :, :, :, : width * UNIT].reshape(d, width * UNIT)

        a = lax.dot_general(weight(0), h[hb], (((0,), (0,)), ((), ())), preferred_element_type=jnp.float32)
        u = gelu(a).astype(jnp.bfloat16)
        return jnp.dot(weight(1), u, preferred_element_type=jnp.float32)

    def group_part(slot, g, hb, pb):
        @pl.when(g == 0)
        def _():
            p[pb] = matmuls(slot, hb, lead)

        @pl.when((g > 0) & (g < groups - 1))
        def _():
            p[pb] = p[pb] + matmuls(slot, hb, GROUP)

        @pl.when(g == groups - 1)
        def _():
            s = p[pb] + matmuls(slot, hb, GROUP)
            h[hb] = (h[hb].astype(jnp.float32) + s).astype(jnp.bfloat16)

    @pl.when(side == 0)
    def _():
        rate = rate_ref[0]
        parts = ((w_up, g_up, nu), (w_dn, g_dn, nd))
        steps = gen + mid

        def chunk_at(s):
            return jnp.where(s % 3 == 2, mid + s // 3, chunk_of(2 * (s // 3) + s % 3))

        def cols_of(c):
            return c // chunks, pl.ds(pl.multiple_of((c % chunks) * UNIT, UNIT), UNIT)

        def loads(s):
            l, cols = cols_of(chunk_at(s))
            slot = s % LOAD_SLOTS
            return [
                pltpu.make_async_copy(r.at[l, :, cols], fin.at[slot, 2 * m + i], lsem.at[slot, 2 * m + i])
                for m in range(2)
                for i, r in enumerate(parts[m][:2])
            ]

        def stores(s):
            l, cols = cols_of(chunk_at(s))
            slot = s % LOAD_SLOTS
            return [
                pltpu.make_async_copy(fnew.at[slot, m], parts[m][2].at[l, :, cols], fsem.at[slot // 2, slot % 2, m])
                for m in range(2)
            ]

        def own_copy(s):
            slot = s % STAGE_SLOTS
            return pltpu.make_async_copy(stage.at[slot], both(mid + s // 3, own), csem.at[slot])

        def post(s):
            slot = s % STAGE_SLOTS
            src = stage.at[slot]
            start(stores(s))

            @pl.when(s % 3 != 2)
            def _():
                e = 2 * (s // 3) + s % 3
                c = chunk_of(e)
                send(src, both(c, own), tss.at[slot, 0], rs.at[Y, c], tp, 1, rep)

                @pl.when(relayed(e))
                def _():
                    send(src, both(c, own), tss.at[slot, 1], rs.at[DG, c], flip_tp, 0, flip_rep)

                @pl.when(e >= RELAY_LAG)
                def _():
                    relay(e - RELAY_LAG)

            @pl.when(s % 3 == 2)
            def _():
                c = mid + s // 3
                own_copy(s).start()
                send(src, both(c, own), tss.at[slot, 0], rs.at[Z, c], flip_tp, 0, rep)
                send(src, both(c, own), tss.at[slot, 1], rs.at[X, c], tp, 0, flip_rep)

        def relay(e):
            @pl.when(relayed(e))
            def _():
                c = chunk_of(e)
                wait(both(c, dia), rs.at[DG, c])
                send(both(c, dia), both(c, dia), ss.at[0, e // chunks], rs.at[DG, c], tp, 1, rep)

        def wait_sent(s):
            slot = s % STAGE_SLOTS
            is_mid = s % 3 == 2
            wait(stage.at[slot], tss.at[slot, 0])

            @pl.when(is_mid | relayed(2 * (s // 3) + s % 3))
            def _():
                wait(stage.at[slot], tss.at[slot, 1])

            @pl.when(is_mid)
            def _():
                own_copy(s).wait()

        def n_stage(f):
            c = mid + f
            wait(both(c, znb), rs.at[Z, c])
            wait(both(c, xnb), rs.at[X, c])

            @pl.when(f % 2 == 0)
            def _():
                send(both(c, znb), both(c, znb), ss.at[2, f // chunks], rs.at[DG, c], tp, 0, flip_rep)

            @pl.when(f % 2 == 1)
            def _():
                send(both(c, xnb), both(c, xnb), ss.at[3, f // chunks], rs.at[DG, c], flip_tp, 0, rep)

        def d_stage(f):
            c = mid + f
            wait(both(c, dia), rs.at[DG, c])
            send(core_half(c, k), core_half(c, k), ss.at[4, f // chunks], rs.at[SB, c], tp, 0, sib_rep)

        for s in range(LOAD_SLOTS - 1):
            start(loads(s))

        def body(s, _):
            @pl.when(s + LOAD_SLOTS - 1 < steps)
            def _():
                start(loads(s + LOAD_SLOTS - 1))

            finish(loads(s))
            slot, lslot = s % STAGE_SLOTS, s % LOAD_SLOTS

            @pl.when(s >= STAGE_SLOTS)
            def _():
                wait_sent(s - STAGE_SLOTS)

            @pl.when(s >= LOAD_SLOTS)
            def _():
                finish(stores(s - LOAD_SLOTS))

            for m in range(2):
                new = fin[lslot, 2 * m] - rate * fin[lslot, 2 * m + 1]
                fnew[lslot, m] = new
                stage[slot, m] = new.astype(jnp.bfloat16)

            @pl.when(s >= 1)
            def _():
                post(s - 1)

            @pl.when(s % 3 == 2)
            def _():
                f = s // 3

                @pl.when(f >= 1)
                def _():
                    n_stage(f - 1)

                @pl.when(f >= 4)
                def _():
                    d_stage(f - 4)

            return 0

        lax.fori_loop(0, steps, body, 0)
        post(steps - 1)
        run(relay, gen - RELAY_LAG, gen)
        n_stage(mid - 1)
        run(wait_sent, steps - STAGE_SLOTS, steps)
        run(d_stage, mid - 4, mid)
        for s in range(steps - LOAD_SLOTS, steps):
            finish(stores(s))
        run(s_wait, mid, 2 * mid)

        def load_group(c, j, slot):
            start(wload(c, slot, j))

        each_chunk(mid, lead, lambda c, j: load_group(c, j, 0))
        per_block = EARLY * groups

        def give_back(b):
            send(h.at[b], h.at[blocks + b], hs.at[b], hr.at[b], tp, 1, rep)

        def visit(t, _):
            b, q = t // per_block, t % per_block
            g, slot = q % groups, q % 2
            each_chunk(0, width_of(g), lambda c, j: finish(wload(c, slot, j)))

            @pl.when(t + 1 < blocks * per_block)
            def _():
                nq = (t + 1) % per_block
                ng = nq % groups
                each_chunk(
                    first_of(EARLY + nq // groups, ng), width_of(ng), lambda c, j: load_group(c, j, 1 - slot)
                )

            @pl.when(q == 0)
            def _():
                @pl.when(b > 0)
                def _():
                    give_back(b - 1)

                wait(h.at[b], hr.at[b])

            group_part(slot, g, b, 0)
            return 0

        lax.fori_loop(0, blocks * per_block, visit, 0)
        run(lambda b: wait(h.at[b], hs.at[b]), 0, blocks - 2)
        give_back(blocks - 1)

        def relay_out(i, _):
            @pl.when(i < pieces)
            def _():
                wait(rin.at[i], rsem.at[0, i])
                send(rin.at[i], rx.at[i], tss.at[0, 0], rsem.at[1, i], flip_tp, 0, rep)

            @pl.when(i >= 1)
            def _():
                q = i - 1
                wait(rx.at[q], rsem.at[1, q])
                send(rx.at[q], out.at[piece_rows(flip_tp, RELAY_BLOCK, q)], tss.at[1, 0],
                     osem.at[RELAY_BLOCK * pieces + q], tp, 1, rep)

            return 0

        lax.fori_loop(0, pieces + 1, relay_out, 0)
        wait(rin, tss.at[0, 0])
        wait(rx, tss.at[1, 0])
        run(lambda b: wait(h.at[b], hs.at[b]), blocks - 2, blocks)
        for l in range(2 * EARLY):
            n = sum(1 for e in range(l * chunks, (l + 1) * chunks) if e % 5 == 4)
            if n:
                wait(wbuf.at[pl.ds(0, n), :, 0, 0, 0], ss.at[0, l])
        for l in range(EARLY):
            for m in range(2):
                n = sum(1 for f in range(l * chunks, (l + 1) * chunks) if f % 2 == m)
                wait(wbuf.at[pl.ds(0, n), :, 0, 0, 0], ss.at[2 + m, l])
            wait(wbuf.at[pl.ds(0, chunks), :, :, 0], ss.at[4, l])

    @pl.when(side == 1)
    def _():
        def y_stage(e):
            c, l = chunk_of(e), e // chunks
            wait(both(c, own), rs.at[Y, c])
            send(both(c, own), both(c, own), ss.at[0, l], rs.at[Z, c], flip_tp, 1, rep)
            send(both(c, own), both(c, own), ss.at[1, l], rs.at[X, c], tp, 1, flip_rep)

        def n_stage(e):
            c, l = chunk_of(e), e // chunks
            wait(both(c, znb), rs.at[Z, c])
            wait(both(c, xnb), rs.at[X, c])
            r = e % 5

            @pl.when((r == 0) | (r == 2))
            def _():
                send(both(c, znb), both(c, znb), ss.at[2, l], rs.at[DG, c], tp, 1, flip_rep)

            @pl.when((r == 1) | (r == 3))
            def _():
                send(both(c, xnb), both(c, xnb), ss.at[3, l], rs.at[DG, c], flip_tp, 1, rep)

        def d_stage(e):
            c = chunk_of(e)
            wait(both(c, dia), rs.at[DG, c])
            send(core_half(c, k), core_half(c, k), ss.at[4, e // chunks], rs.at[SB, c], tp, 1, sib_rep)

        turn = EARLY * groups * blocks

        def front(i, t):
            a, s1, jump, s2 = FRONTS[i]
            late = jump + (s1 * turn) // 16 + (s2 * (t - turn)) // 16
            return jnp.minimum(gen, a + jnp.where(t <= turn, (s1 * t) // 16, late))

        def pload(b):
            rows = pl.ds(pl.multiple_of(tp * my_rows + b * BLOCK, BLOCK), BLOCK)
            return pltpu.make_async_copy(prompts.at[rows], rows_buf.at[b % 2], iosem.at[b % 2])

        pload(0).start()
        for b in range(blocks):
            if b + 1 < blocks:
                pload(b + 1).start()
            pload(b).wait()
            for j in range(pieces):
                h[b, :, pl.ds(j * PIECE, PIECE)] = rows_buf[b % 2, pl.ds(j * PIECE, PIECE), :].T

        n_pro = FRONTS[0][0]
        for e in range(n_pro):
            y_stage(e)
            for i, fn in ((1, n_stage), (2, d_stage)):
                if e >= n_pro - FRONTS[i][0]:
                    fn(e - (n_pro - FRONTS[i][0]))
            j = e - (n_pro - lead)
            if j >= 0:
                s_wait(j)
                start(wload(j, 0, j))

        def put(b, j):
            src = rows_buf.at[b % 2, pl.ds(j * PIECE, PIECE), :]
            rows = piece_rows(tp, b, j)
            pltpu.make_async_copy(src, out.at[rows], psem.at[b % 2, j, 0]).start()

            @pl.when(b == RELAY_BLOCK)
            def _():
                send(src, rin.at[j], psem.at[b % 2, j, 1], rsem.at[0, j], tp, 0, rep)

            @pl.when(b != RELAY_BLOCK)
            def _():
                send(src, out.at[rows], psem.at[b % 2, j, 1], osem.at[b * pieces + j], flip_tp, 1, rep)

        def put_wait(b):
            for j in range(pieces):
                src = rows_buf.at[b % 2, pl.ds(j * PIECE, PIECE), :]
                wait(src, psem.at[b % 2, j, 0])
                wait(src, psem.at[b % 2, j, 1])

        wide = turn - (groups // 2) * blocks
        n_late = EARLY * groups * blocks
        paired = FIRST_LATE + 2 * (blocks - FIRST_LATE)
        first_late, last_late = 2 * EARLY, 2 * EARLY + 1

        def late_task(q):
            j = (q - FIRST_LATE) // 2
            in_pairs = (q >= FIRST_LATE) & (q < paired)
            last = jnp.where(in_pairs, (q - FIRST_LATE) % 2 == 0, q >= paired)
            b = jnp.where(in_pairs, jnp.where(last, j, j + FIRST_LATE), jnp.where(q < FIRST_LATE, q, q - blocks))
            return jnp.where(last, last_late, first_late), b

        def give(b):
            send(h.at[b], h.at[b], hs.at[b], hr.at[b], tp, 0, rep)

        def visit(t, _):
            late = t >= turn
            split = (t >= wide) & (t < turn)
            tl, tb = late_task((t - turn) // groups)
            per_layer = groups * blocks
            l = jnp.where(late, tl, jnp.where(split, EARLY - 1, t // per_layer))
            half = groups // 2
            g = jnp.where(late, t % groups, jnp.where(split, half + (t - wide) % half, (t // blocks) % groups))
            b = jnp.where(late, tb, jnp.where(split, (t - wide) // half, t % blocks))
            slot = g % 2
            hb = jnp.where(late, blocks + b, b)
            width = width_of(g)

            @pl.when(late | (b == 0))
            def _():
                each_chunk(0, width, lambda c, j: finish(wload(c, slot, j)))

            @pl.when(t < turn + FIRST_LATE * groups)
            def _():
                for i, fn in enumerate((y_stage, n_stage, d_stage)):
                    run(fn, front(i, t), front(i, t + 1))

            @pl.when((t > wide) & (t <= turn) & (g % half == 0))
            def _():
                give((t - wide) // half - 1)

            @pl.when(t < wide)
            def _():
                @pl.when(b < jnp.where(g == groups - 1, lead, GROUP))
                def _():
                    c = first_of(l, g) + width + b
                    s_wait(c)
                    start(wload(c, 1 - slot, b))

            @pl.when(t == turn - 1)
            def _():
                run(lambda e: s_wait(chunk_of(e)), mid, mid + chunks)

            @pl.when(t == turn + FIRST_LATE * groups - 1)
            def _():
                for i, fn in enumerate((y_stage, n_stage, d_stage)):
                    run(fn, front(i, t + 1), gen)
                run(lambda e: s_wait(chunk_of(e)), mid + chunks, gen)

            @pl.when((t == wide) | ((t >= turn - 1) & (t + 1 < turn + n_late)))
            def _():
                ntl, _ = late_task((t + 1 - turn) // groups)
                nl = jnp.where(t == wide, EARLY - 1, ntl)
                ng = jnp.where(t == wide, groups - 1, (t + 1) % groups)

                def fetch(c, j):
                    @pl.when(t == wide)
                    def _():
                        s_wait(c)

                    start(wload(c, 1 - slot, j))

                each_chunk(first_of(nl, ng), width_of(ng), fetch)

            @pl.when(late & (l == first_late) & (g == 0))
            def _():
                wait(h.at[hb], hr.at[b])

            group_part(slot, g, hb, b)

            @pl.when((l == last_late) & (g == groups - 1))
            def _():
                @pl.when(b >= 2)
                def _():
                    put_wait(b - 2)

                for j in range(pieces):
                    cols = pl.ds(j * PIECE, PIECE)
                    rows_buf[b % 2, cols, :] = h[hb, :, cols].T
                    if j >= 1:
                        put(b, j - 1)
                put(b, pieces - 1)

            return 0

        lax.fori_loop(0, turn + n_late, visit, 0)
        for b in range(blocks - 2, blocks):
            put_wait(b)
        run(lambda b: wait(h.at[b], hs.at[b]), 0, blocks)
        for i in range(blocks * pieces):
            wait(out.at[piece_rows(flip_tp, i // pieces, i % pieces)], osem.at[i])
        for l in range(2 * EARLY):
            for i in range(5):
                if i == 4:
                    wait(wbuf.at[pl.ds(0, chunks), :, :, 0], ss.at[i, l])
                else:
                    es = range(l * chunks, (l + 1) * chunks)
                    n = sum(1 for e in es if i < 2 or e % 5 in ((0, 2), (1, 3))[i - 2])
                    wait(wbuf.at[pl.ds(0, n), :, 0, 0, 0], ss.at[i, l])


def finish_kernel(up, dn, rows, new_up, new_dn, out, buf, zbuf, lsem, ssem, zsem):
    layers = up.shape[0]
    n_rows = rows.shape[0]
    slots, band, hidden = buf.shape
    side = lax.axis_index("side")
    items = [(i, o, l) for l in range(layers) for i, o in ((up, new_up), (dn, new_dn))]
    piece = zbuf.shape[1]
    n_pieces = n_rows // piece
    n_slots = zbuf.shape[0]

    def pipeline(n, n_slots, load, store):
        for i in range(min(n_slots, n)):
            load(i).start()
        half = n_slots // 2
        for i in range(n):
            load(i).wait()
            store(i).start()
            nxt = i + half
            if i >= half and nxt < n:
                store(nxt - n_slots).wait()
                load(nxt).start()

    @pl.when(side == 0)
    def _():
        zbuf[0] = jnp.zeros(zbuf.shape[1:], zbuf.dtype)
        zeros = [
            pltpu.make_async_copy(zbuf.at[0], out.at[pl.ds(i * piece, piece)], zsem.at[i]) for i in range(n_pieces)
        ]
        for cp in zeros:
            cp.start()

        def load(i):
            src, _, l = items[i]
            return pltpu.make_async_copy(src.at[l], buf.at[i % slots], lsem.at[i % slots])

        def store(i):
            _, dst, l = items[i]
            return pltpu.make_async_copy(buf.at[i % slots], dst.at[l], ssem.at[i % slots])

        n = len(items)
        pipeline(n, slots, load, store)
        for i in range(max(n - slots, 0), n):
            store(i).wait()
        for cp in zeros:
            cp.wait()

    @pl.when(side == 1)
    def _():
        buf[0] = jnp.zeros(buf.shape[1:], buf.dtype)
        zeros = [pltpu.make_async_copy(buf.at[0], dst.at[l], zsem.at[i]) for i, (_, dst, l) in enumerate(items)]
        for cp in zeros:
            cp.start()

        def load(i):
            return pltpu.make_async_copy(rows.at[pl.ds(i * piece, piece)], zbuf.at[i % n_slots], lsem.at[i % n_slots])

        def store(i):
            return pltpu.make_async_copy(zbuf.at[i % n_slots], out.at[pl.ds(i * piece, piece)], ssem.at[i % n_slots])

        pipeline(n_pieces, n_slots, load, store)
        for i in range(max(n_pieces - n_slots, 0), n_pieces):
            store(i).wait()
        for cp in zeros:
            cp.wait()


def solution(mesh):
    up_spec = P("side", None, ("rep", "tp"), None)
    down_spec = P("side", None, None, ("rep", "tp"))
    tok_spec = P("side", "rep", None, None)

    def device_step(w_up, w_down, g_up, g_down, learn_rate, prompts):
        layers, band, hidden = w_up.shape[1:]
        n_rows, d = prompts.shape[2:]
        chunks = hidden // UNIT
        total = layers * chunks
        my_rows = n_rows // 2
        blocks, pieces = my_rows // BLOCK, BLOCK // PIECE
        weights = (w_up[0], jnp.swapaxes(w_down[0], 1, 2), g_up[0], jnp.swapaxes(g_down[0], 1, 2))
        smem = pl.BlockSpec(memory_space=pltpu.SMEM)
        hbm = pl.BlockSpec(memory_space=pl.ANY)
        bf16 = jnp.bfloat16
        relay = jax.ShapeDtypeStruct((pieces, PIECE, d), bf16)
        new_w = jax.ShapeDtypeStruct((layers, band, hidden), jnp.float32)
        rows = jax.ShapeDtypeStruct((n_rows, d), bf16)
        rows_mid, up_mid, dn_mid, _, _, _ = pl.pallas_call(
            sync_kernel,
            name="sync_and_forward",
            out_shape=(
                rows,
                new_w,
                new_w,
                jax.ShapeDtypeStruct((total, 2, 2, 2, 2, band, UNIT), bf16),
                relay,
                relay,
            ),
            in_specs=[smem] + [hbm] * 5,
            out_specs=(hbm,) * 6,
            scratch_shapes=[
                pltpu.VMEM((2 * blocks, d, BLOCK), bf16),
                pltpu.VMEM((blocks, d, BLOCK), jnp.float32),
                pltpu.VMEM((2, 2, 2, 2, 2, band, GROUP * UNIT), bf16),
                pltpu.VMEM((LOAD_SLOTS, 4, band, UNIT), jnp.float32),
                pltpu.VMEM((LOAD_SLOTS, 2, band, UNIT), jnp.float32),
                pltpu.VMEM((STAGE_SLOTS, 2, band, UNIT), bf16),
                pltpu.VMEM((2, BLOCK, d), bf16),
                pltpu.SemaphoreType.DMA((5, total)),
                pltpu.SemaphoreType.DMA((5, 2 * EARLY)),
                pltpu.SemaphoreType.DMA((LOAD_SLOTS, 4)),
                pltpu.SemaphoreType.DMA((2, GROUP, 2)),
                pltpu.SemaphoreType.DMA((STAGE_SLOTS, 2)),
                pltpu.SemaphoreType.DMA((STAGE_SLOTS,)),
                pltpu.SemaphoreType.DMA((2,)),
                pltpu.SemaphoreType.DMA((2, pieces, 2)),
                pltpu.SemaphoreType.DMA((blocks * pieces,)),
                pltpu.SemaphoreType.DMA((2, pieces)),
                pltpu.SemaphoreType.DMA((blocks,)),
                pltpu.SemaphoreType.DMA((blocks,)),
            ],
            compiler_params=pltpu.CompilerParams(has_side_effects=True, vmem_limit_bytes=60 * 1024 * 1024),
        )(learn_rate, *weights, prompts[0, 0])
        new_up, new_dn, gen_out = pl.pallas_call(
            finish_kernel,
            name="write_outputs",
            out_shape=(new_w, new_w, rows),
            in_specs=[hbm] * 3,
            out_specs=(hbm,) * 3,
            scratch_shapes=[
                pltpu.VMEM((8, band, hidden), jnp.float32),
                pltpu.VMEM((8, n_rows // 16, d), bf16),
                pltpu.SemaphoreType.DMA((8,)),
                pltpu.SemaphoreType.DMA((8,)),
                pltpu.SemaphoreType.DMA((max(16, 2 * layers),)),
            ],
            compiler_params=pltpu.CompilerParams(vmem_limit_bytes=62 * 1024 * 1024),
        )(up_mid, dn_mid, rows_mid)
        return new_up[None], jnp.swapaxes(new_dn, 1, 2)[None], gen_out[None, None]

    return jax.shard_map(
        device_step,
        mesh=mesh,
        in_specs=(up_spec, down_spec, up_spec, down_spec, P("side"), tok_spec),
        out_specs=(up_spec, down_spec, tok_spec),
        check_vma=False,
    )
```

time: 620 us -> 560 us (0.903)
  Pallas kernels: 618 us -> 558 us
    pallas_call x1, Pallas kernels: 595 us -> 535 us  [device_step(): pl.pallas_call(sync_kernel, name='sync_and_forward', out_shape=(rows, new...]
where the time goes in v5:
time: 560 us
  Pallas kernels  558 us (100%)
    pallas_call x1, Pallas kernels, device_step(): pl.pallas_call(sync_kernel, name='sync_and_forward', out_shape=(rows, new...  535 us
    pallas_call x1, Pallas kernels, device_step(): pl.pallas_call(finish_kernel, name='write_outputs', out_shape=(new_w, new...  23.2 us

profile of v5, /device:TPU:0, one launch (start us, length us, event | category | flops | bytes accessed | tf_op | source)
XLA Modules:
  0.0 559.8 jit_solution(10257754980856238109)
XLA Ops:
  1.3 535.1 %sync_and_forward.1 = (bf16[8192,896]{1,0:T(8,128)(2,1)}, f32[6,112,4864]{2,1,0:T(8,128)}, f32[6,112,4864]{2,1,0:T(8,128)}, bf16[114,2,2,2,2,112,256]{6,5,4,3,2,...) custom-call(f32[1]{0:T(128)S(6)} %copy.9.rate_ref, f32[6,112,4864]{2,1,0:T(8,128)} %bitcast.15, ...), custom_call_target="tpu_custom_call" | custom-call | tf_op jit(solution)/shard_map/sync_and_forward/pallas_call | solution.py:627
  536.4 23.2 %write_outputs.1 = (f32[6,112,4864]{2,1,0:T(8,128)}, f32[6,112,4864]{2,1,0:T(8,128)}, bf16[8192,896]{1,0:T(8,128)(2,1)}) custom-call(f32[6,112,4864]{2,1,0:T(8,128)} %get-tuple-element.9.up, f32[6,112,4864]{2,1,0:T(8,128)} %get-tuple-element.10.dn, bf16[8192,896]{1,0:T(8,128)(2,1)} %get-tuple-element.11.rows), custom_call_target="tpu_custom_call" | custom-call | tf_op jit(solution)/shard_map/write_outputs/pallas_call | solution.py:663
